TPU v7x, 8 devices: a whole 2x2x1 slice. The times are simulated.
8 devices in a mesh: dp: 1 (over z), col: 2 (over y), row: 4 (over x, core).
Axes of the slice: x: 2, y: 2, z: 1, core: 2. Of those that a mesh axis runs over, the one named last changes fastest.
Arguments:
- act_in: bfloat16 [8192, 8192], P(('dp', 'row'), 'col')
- w_down: bfloat16 [8192, 2048], P('row', 'col')
- grad_out: bfloat16 [8192, 2048], P(('dp', 'row'), 'col')
Outputs:
- output 1: bfloat16 [8192, 8192], P(('dp', 'row'), 'col')
- output 2: float32 [8192, 2048], P(('dp', 'row'), 'col')
All inputs are finite; a program needn't handle non-finite values.
Results may differ from a plain program's by a relative error of at most 0.001.
Values are sent between devices in bfloat16 or wider.
A program may use at most 1 GiB of HBM per device.

v0:
```python
import jax
import jax.numpy as jnp
from jax import lax
from jax.sharding import PartitionSpec as P


def solution(mesh):
    io_spec = P(("dp", "row"), "col")
    w_spec = P("row", "col")

    def local_backward(act_blk, w_blk, grad_blk):
        w_cols = lax.all_gather(w_blk, "row", axis=0, tiled=True)
        grad_in_part = jnp.einsum("tn,kn->tk", grad_blk, w_cols, preferred_element_type=jnp.float32)
        grad_in = lax.psum_scatter(grad_in_part, "col", scatter_dimension=1, tiled=True).astype(jnp.bfloat16)
        act_rows = lax.all_gather(act_blk, "col", axis=1, tiled=True)
        grad_w_part = jnp.einsum("tk,tn->kn", act_rows, grad_blk, preferred_element_type=jnp.float32)
        grad_w = lax.psum_scatter(grad_w_part, "row", scatter_dimension=0, tiled=True)
        return grad_in, grad_w

    return jax.shard_map(local_backward, mesh=mesh, in_specs=(io_spec, w_spec, io_spec), out_specs=(io_spec, io_spec), check_vma=False)
```

profile of v0, /device:TPU:0, one launch (start us, length us, event | category | flops | bytes accessed | tf_op | source)
XLA Modules:
  0.0 1467.1 jit_solution(10053127843386960311)
XLA Ops:
  7.2 0.0 all-gather.3.cloned.1.call-start
  7.2 0.7 all-gather.3.cloned.1.call-update
  7.9 0.0 all-gather.5.cloned.1.call-start
  7.9 0.7 all-gather.5.cloned.1.call-update
  8.6 0.0 reduce-scatter.3.cloned.1.call-start
  8.7 107.9 %all-gather.3.cloned.1.call-done = bf16[8192,1024]{1,0:T(8,128)(2,1)} async-done(((bf16[2048,1024]{1,0:T(8,128)(2,1)}), bf16[8192,1024]{1,0:T(8,128)(2,1)}) %all-gather.3.cloned.1.call-update) | async-done | bytes 16777232 | tf_op jit(solution)/shard_map/all_gather | solution.py:12
  116.5 45.0 %fusion = f32[2048,8192]{1,0:T(8,128)} fusion(bf16[2048,1024]{1,0:T(8,128)(2,1)} %param.5, bf16[8192,1024]{1,0:T(8,128)(2,1)} %all-gather.3.cloned.1.call-done), kind=kOutput, calls=%fused_computation | convolution fusion | flops 34359738368 | bytes 88080384 | tf_op jit(solution)/shard_map/tn,kn->tk/dot_general | solution.py:13
  161.5 0.0 reduce-scatter.3.cloned.1.call-update
  161.6 0.2 reduce-scatter.5.cloned.1.call-start
  161.8 341.8 %all-gather.5.cloned.1.call-done = bf16[2048,8192]{1,0:T(8,128)(2,1)} async-done(((bf16[2048,4096]{1,0:T(8,128)(2,1)}), bf16[2048,8192]{1,0:T(8,128)(2,1)}) %all-gather.5.cloned.1.call-update) | async-done | bytes 33554448 | tf_op jit(solution)/shard_map/all_gather | solution.py:15
  503.6 42.1 %fusion.1 = f32[8192,1024]{1,0:T(8,128)} fusion(bf16[2048,8192]{1,0:T(8,128)(2,1)} %all-gather.5.cloned.1.call-done, bf16[2048,1024]{1,0:T(8,128)(2,1)} %param.5), kind=kOutput, calls=%fused_computation.1 | convolution fusion | flops 34359738368 | bytes 71303168 | tf_op jit(solution)/shard_map/tk,tn->kn/dot_general | solution.py:16
  545.7 0.0 reduce-scatter.5.cloned.1.call-update
  545.7 685.8 %reduce-scatter.3.cloned.1.call-done = f32[2048,4096]{1,0:T(8,128)} async-done(((f32[2048,8192]{1,0:T(8,128)}), f32[2048,4096]{1,0:T(8,128)}) %reduce-scatter.3.cloned.1.call-update) | async-done | bytes 33554448 | tf_op jit(solution)/shard_map/reduce_scatter | solution.py:14
  1231.5 17.4 %convert_element_type.3 = bf16[2048,4096]{1,0:T(8,128)(2,1)} convert(f32[2048,4096]{1,0:T(8,128)} %reduce-scatter.3.cloned.1.call-done) | non-fusion elementwise | flops 8388608 | bytes 50331648 | tf_op jit(solution)/shard_map/convert_element_type | solution.py:14
  1248.9 211.7 %reduce-scatter.5.cloned.1.call-done = f32[2048,1024]{1,0:T(8,128)} async-done(((f32[8192,1024]{1,0:T(8,128)}), f32[2048,1024]{1,0:T(8,128)}) %reduce-scatter.5.cloned.1.call-update) | async-done | bytes 8388624 | tf_op jit(solution)/shard_map/reduce_scatter | solution.py:17
Async XLA Ops:
  7.2 109.4 %all-gather.3.cloned.1.call-start = ((), (), s32[]{:S(2)}) async-start(), calls=%async_computation.2 | async-start | bytes 20971520 | tf_op jit(solution)/shard_map/all_gather | solution.py:12
  7.9 495.7 %all-gather.5.cloned.1.call-start = ((), (), s32[]{:S(2)}) async-start(), calls=%async_computation.4 | async-start | bytes 50331648 | tf_op jit(solution)/shard_map/all_gather | solution.py:15
  8.6 1222.9 %reduce-scatter.3.cloned.1.call-start = ((), (), s32[]{:S(2)}) async-start(), calls=%async_computation.3 | async-start | bytes 100663296 | tf_op jit(solution)/shard_map/reduce_scatter | solution.py:14
  161.6 1299.0 %reduce-scatter.5.cloned.1.call-start = ((), (), s32[]{:S(2)}) async-start(), calls=%async_computation.5 | async-start | bytes 41943040 | tf_op jit(solution)/shard_map/reduce_scatter | solution.py:17
Sparse Core Ops, SparseCore 0:
  9.5 107.0 all-gather.2
  118.1 385.4 all-gather.4
  505.9 725.6 reduce-scatter.2
  1234.5 226.0 reduce-scatter.4
where the time goes:
time: 1470 us
  waiting for transfers between devices  1350 us (92%)
  matrix products  87.1 us (6%)
  other arithmetic  17.4 us (1%)
    reduce_scatter x1, waiting for transfers between devices, local_backward(): lax.psum_scatter(grad_in_part, 'col', scatter_dimension=1, tiled=True)  686 us
    all_gather x1, waiting for transfers between devices, local_backward(): act_rows = lax.all_gather(act_blk, 'col', axis=1, tiled=True)  342 us
    reduce_scatter x1, waiting for transfers between devices, local_backward(): lax.psum_scatter(grad_w_part, 'row', scatter_dimension=0, tiled=True)  212 us
    all_gather x1, waiting for transfers between devices, local_backward(): w_cols = lax.all_gather(w_blk, 'row', axis=0, tiled=True)  108 us
    dot_general x1, matrix products, local_backward(): jnp.einsum('tn,kn->tk', grad_blk, w_cols, preferred_element_type=jnp.floa...  45 us
    dot_general x1, matrix products, local_backward(): jnp.einsum('tk,tn->kn', act_rows, grad_blk, preferred_element_type=jnp.fl...  42.1 us
  transfers between devices with their start and end apart: 4, of which 4 were waited for; matrix products, arithmetic and copies ran while one was open for 7% of the time, Pallas kernels for 0%

commit v1 on v0

v1 whole, which is shorter than its diff:
```python
import functools

import jax
import jax.numpy as jnp
from jax import lax
from jax.experimental import pallas as pl
from jax.experimental.pallas import tpu as pltpu
from jax.sharding import PartitionSpec as P

MESH = pl.DeviceIdType.MESH
F32 = jnp.float32
BF16 = jnp.bfloat16


def _tdot(a, b):
    return lax.dot_general(a, b, (((0,), (0,)), ((), ())), preferred_element_type=F32)


def _dot_t(a, b):
    return lax.dot_general(a, b, (((1,), (1,)), ((), ())), preferred_element_type=F32)


def kernel(
    x_ref, w_ref, dy_ref,
    dx_ref, dw_ref, wbuf, bufx, bufy,
    dyv, xo, xs, pown, poth, wv, xv, lb,
    ld_sem, dys_r, dyy_r, xs_r, w_r, ws_r, px_r, py_r,
    s_dys, s_dyy, s_xs, s_w, s_ws, s_px, s_py, s_sum,
    wl_sem, xv_sem, lb_sem, out_sem,
):
    row = lax.axis_index("row")
    y = lax.axis_index("col")
    x = row // 2
    c = row % 2
    is_a = x == y
    is_b = x != y
    sib = {"row": row + 1 - 2 * c}
    xn = {"row": (row + 2) % 4}
    yn = {"col": 1 - y}

    def remote(src, dst, ssem, rsem, dev):
        return pltpu.make_async_remote_copy(
            src_ref=src, dst_ref=dst, send_sem=ssem, recv_sem=rsem, device_id=dev, device_id_type=MESH
        )

    def local(src, dst, sem):
        return pltpu.make_async_copy(src, dst, sem)

    def qs(q):
        return pl.ds(q * 256, 256)

    barrier = pltpu.get_barrier_semaphore()
    for dev in (sib, xn, yn):
        pl.semaphore_signal(barrier, inc=1, device_id=dev, device_id_type=MESH)
    pl.semaphore_wait(barrier, 3)

    def dy_to_sib(j, q):
        src = dy_ref.at[:, qs(q)] if j == 0 else dyv.at[0, 1, :, qs(q)]
        return remote(src, dyv.at[1, j, :, qs(q)], s_dys.at[0], dys_r.at[j, q], sib)

    def dy_to_y(q):
        return remote(dy_ref.at[:, qs(q)], dyv.at[0, 1, :, qs(q)], s_dyy.at[0], dyy_r.at[q], yn)

    def x_load(kt):
        return local(x_ref.at[:, pl.ds(c * 2048 + kt * 512, 512)], xo.at[kt], ld_sem.at[1 + kt])

    def x_to_sib(kt):
        return remote(
            x_ref.at[:, pl.ds((1 - c) * 2048 + kt * 512, 512)], xs.at[kt], s_xs.at[0], xs_r.at[kt], sib
        )

    def rows(i):
        return pl.ds(i * 256, 256)

    def w_own_to_x(i):
        return remote(w_ref.at[rows(i)], wbuf.at[0, 0, rows(i)], s_w.at[0], w_r.at[0, i], xn)

    def w_to_y(i):
        return remote(w_ref.at[rows(i)], wbuf.at[0, 1, rows(i)], s_w.at[0], w_r.at[1, i], yn)

    def w_fwd(i):
        return remote(wbuf.at[0, 1, rows(i)], wbuf.at[0, 1, rows(i)], s_w.at[0], w_r.at[1, i], xn)

    def w_to_sib(j, i, own):
        src = w_ref.at[rows(i)] if own else wbuf.at[0, j, rows(i)]
        return remote(src, wbuf.at[1, j, rows(i)], s_ws.at[0], ws_r.at[j, i], sib)

    def p_to_x(g, src, q, kt):
        return remote(src.at[q, kt], bufx.at[g, q % 2, kt], s_px.at[0], px_r.at[g * 8 + (q % 2) * 4 + kt], xn)

    def p_to_y_half(q, kt, h):
        part = pl.ds(h * 256, 256)
        return remote(
            poth.at[q, kt, part], bufy.at[q, kt, part], s_py.at[0], py_r.at[q * 8 + kt * 2 + h], yn
        )

    def p_fwd(i):
        q, kt, h = i // 8, (i // 2) % 4, i % 2
        part = pl.ds(h * 256, 256)
        return remote(bufy.at[q, kt, part], bufx.at[0, q, kt, part], s_px.at[0], px_r.at[i], xn)

    def p_term(q, kt):
        return remote(poth.at[q, kt], bufy.at[q, kt], s_py.at[0], py_r.at[q * 4 + kt], yn)

    def sum_to_y(q, kt):
        return remote(
            poth.at[q, kt], dw_ref.at[pl.ds(kt * 512, 512), qs(q)], s_sum.at[0],
            py_r.at[8 + (q - 2) * 4 + kt], yn,
        )

    dy_load = local(dy_ref, dyv.at[0, 0], ld_sem.at[0])
    dy_to_sib(0, 0).start()
    dy_to_y(0).start()
    dy_load.start()
    x_to_sib(0).start()
    x_load(0).start()

    @pl.when(is_a)
    def _():
        for i in range(8):
            w_own_to_x(i).start()
        for q in range(1, 4):
            dy_to_y(q).start()

    @pl.when(is_b)
    def _():
        dy_to_y(1).start()
        for i in range(6):
            w_to_y(i).start()
        dy_to_y(2).start()
        for i in range(6, 8):
            w_to_y(i).start()
        dy_to_y(3).start()

    for kt in range(1, 4):
        x_to_sib(kt).start()
        x_load(kt).start()
    for q in range(1, 4):
        dy_to_sib(0, q).start()

    @pl.when(is_a)
    def _():
        for i in range(8):
            w_to_sib(0, i, True).start()

    def p_tile(dst, j, q, kt):
        dst[q, kt] = _tdot(xo[kt], dyv[0, j, :, q * 256:(q + 1) * 256]) + _tdot(
            xs[kt], dyv[1, j, :, q * 256:(q + 1) * 256]
        )

    dy_load.wait()
    for q in range(4):
        dy_to_sib(0, q).wait_recv()

        def own_body(kt, carry, q=q):
            if q == 0:
                x_load(kt).wait()
                x_to_sib(kt).wait_recv()
            p_tile(pown, 0, q, kt)
            if q < 2:
                @pl.when(is_b)
                def _():
                    p_to_x(0, pown, q, kt).start()
            return carry

        lax.fori_loop(0, 4, own_body, 0)

    def other_pass(q):
        dy_to_y(q).wait_recv()
        dy_to_sib(1, q).start()
        dy_to_sib(1, q).wait_recv()

        def body(kt, carry):
            p_tile(poth, 1, q, kt)
            if q < 2:
                @pl.when(is_a)
                def _():
                    p_term(q, kt).start()

                @pl.when(is_b)
                def _():
                    p_to_y_half(q, kt, 0).start()
                    p_to_y_half(q, kt, 1).start()
            else:
                @pl.when(is_b)
                def _():
                    p_to_x(1, poth, q, kt).start()
            return carry

        lax.fori_loop(0, 4, body, 0)

    def a_final(g, t):
        q2, kt = t // 4, t % 4
        q = q2 + (0 if g == 0 else 2)
        p_to_x(g, pown, q, kt).wait_recv()
        ld = local(bufx.at[g, q2, kt], lb.at[0], lb_sem.at[0])
        ld.start()
        ld.wait()
        pown[q, kt] = pown[q, kt] + lb[0]
        local(pown.at[q, kt], dw_ref.at[pl.ds(kt * 512, 512), qs(q)], out_sem.at[0]).start()

    def a_sum(q, kt):
        p_to_x(1, poth, q, kt).wait_recv()
        ld = local(bufx.at[1, q % 2, kt], lb.at[1], lb_sem.at[1])
        ld.start()
        ld.wait()
        poth[q, kt] = poth[q, kt] + lb[1]
        sum_to_y(q, kt).start()

    def w_fwd_step(i):
        w_to_y(i).wait_recv()
        w_fwd(i).start()
        w_to_sib(1, i, False).start()

    def w_loads(e, own_from_arg):
        cc, d = e % 2, e // 2
        slot = e % 2
        if own_from_arg:
            first = local(w_ref.at[rows(d)], wv.at[slot, 0], wl_sem.at[slot, 0])
        else:
            first = local(wbuf.at[cc, 0, rows(d)], wv.at[slot, 0], wl_sem.at[slot, 0])
        return first, local(wbuf.at[cc, 1, rows(d)], wv.at[slot, 1], wl_sem.at[slot, 1])

    def xv_out(d, cc):
        k0 = (c + cc * (1 - 2 * c)) * 2048
        return local(xv.at[cc], dx_ref.at[:, pl.ds(k0 + d * 256, 256)], xv_sem.at[cc])

    def dx_stripe(d, cc):
        @pl.when(d > 0)
        def _():
            xv_out(d, cc).wait()

        def body(m, carry):
            part = pl.ds(m * 512, 512)
            xv[cc, part, :] = (
                _dot_t(dyv[0, 0, part, :], wv[cc, 0]) + _dot_t(dyv[0, 1, part, :], wv[cc, 1])
            ).astype(BF16)
            return carry

        lax.fori_loop(0, 4, body, 0)
        xv_out(d, cc).start()

    def start_loads(d, cc, own_from_arg):
        for cp in w_loads(2 * d + cc, own_from_arg):
            cp.start()

    def wait_loads(d, cc, own_from_arg):
        for cp in w_loads(2 * d + cc, own_from_arg):
            cp.wait()

    other_pass(0)
    other_pass(1)

    @pl.when(is_a)
    def _():
        def body(i, carry):
            w_fwd_step(i)
            a_final(0, i)
            return carry

        lax.fori_loop(0, 6, body, 0)

    other_pass(2)

    @pl.when(is_a)
    def _():
        def body(i, carry):
            w_fwd_step(i)
            a_final(0, i)
            a_sum(2, 2 * (i - 6))
            a_sum(2, 2 * (i - 6) + 1)
            return carry

        lax.fori_loop(6, 8, body, 0)

    other_pass(3)

    @pl.when(is_a)
    def _():
        def sib_wait(d):
            w_to_sib(0, d, True).wait_recv()
            w_to_sib(1, d, False).wait_recv()

        start_loads(0, 0, True)

        def body(d, carry):
            p_to_y_half(d // 4, d % 4, 0).wait_recv()
            p_fwd(2 * d).start()
            sib_wait(d)
            start_loads(d, 1, False)
            wait_loads(d, 0, True)
            dx_stripe(d, 0)

            @pl.when(d < 4)
            def _():
                a_sum(3, d)

            p_to_y_half(d // 4, d % 4, 1).wait_recv()
            p_fwd(2 * d + 1).start()

            @pl.when(d < 7)
            def _():
                start_loads(d + 1, 0, True)

            wait_loads(d, 1, False)
            dx_stripe(d, 1)

            @pl.when(d >= 2)
            def _():
                a_final(2, d - 2)
            return carry

        lax.fori_loop(0, 8, body, 0)
        a_final(2, 6)
        a_final(2, 7)
        for cc in range(2):
            xv_out(7, cc).wait()
        local(dw_ref, dw_ref, out_sem.at[0]).wait()
        remote(wbuf.at[0], wbuf.at[0], s_w.at[0], w_r.at[0, 0], xn).wait_send()
        remote(bufx.at[0], bufx.at[0], s_px.at[0], px_r.at[0], xn).wait_send()
        remote(bufy, bufy, s_py.at[0], py_r.at[0], yn).wait_send()
        remote(bufy, bufy, s_sum.at[0], py_r.at[0], yn).wait_send()

    @pl.when(is_b)
    def _():
        for q in range(2, 4):
            for kt in range(4):
                p_to_x(2, pown, q, kt).start()

        def own_w(i, carry):
            w_own_to_x(i).wait_recv()
            w_to_sib(0, i, False).start()
            return carry

        lax.fori_loop(0, 8, own_w, 0)

        def body(d, carry):
            w_to_y(d).wait_recv()
            w_to_sib(1, d, False).start()
            start_loads(d, 0, False)
            w_to_sib(0, d, False).wait_recv()
            w_to_sib(1, d, False).wait_recv()
            start_loads(d, 1, False)
            wait_loads(d, 0, False)
            dx_stripe(d, 0)
            wait_loads(d, 1, False)
            dx_stripe(d, 1)
            return carry

        lax.fori_loop(0, 8, body, 0)

        def out_half(q, kt, h, slot):
            return local(
                lb.at[2 + slot, pl.ds(0, 256)],
                dw_ref.at[pl.ds(kt * 512 + h * 256, 256), pl.ds(q * 256, 256)],
                out_sem.at[slot],
            )

        def fin(i, carry):
            q, kt = i // 4, i % 4
            p_term(q, kt).wait_recv()
            for h in range(2):
                part = pl.ds(h * 256, 256)
                first = local(bufy.at[q, kt, part], lb.at[h, pl.ds(0, 256)], lb_sem.at[h])
                first.start()
                p_fwd(i * 2 + h).wait_recv()
                second = local(bufx.at[0, q, kt, part], lb.at[h, pl.ds(256, 256)], lb_sem.at[2 + h])
                second.start()

                @pl.when(i > 0)
                def _():
                    out_half(q, kt, h, h).wait()

                first.wait()
                second.wait()
                lb[2 + h, 0:256] = lb[h, 0:256] + lb[h, 256:512]
                out_half(q, kt, h, h).start()
            return carry

        lax.fori_loop(0, 8, fin, 0)
        for q in range(2, 4):
            for kt in range(4):
                sum_to_y(q, kt).wait_recv()
        for h in range(2):
            out_half(1, 3, h, h).wait()
        for cc in range(2):
            xv_out(7, cc).wait()
        remote(wbuf.at[0, 0], wbuf.at[0, 0], s_w.at[0], w_r.at[0, 0], yn).wait_send()
        remote(bufx, bufx, s_px.at[0], px_r.at[0], xn).wait_send()
        remote(bufy, bufy, s_py.at[0], py_r.at[0], yn).wait_send()

    remote(dyv.at[0], dyv.at[0], s_dys.at[0], dys_r.at[0, 0], sib).wait_send()
    remote(dyv.at[0, 0], dyv.at[0, 0], s_dyy.at[0], dyy_r.at[0], yn).wait_send()
    remote(xs, xs, s_xs.at[0], xs_r.at[0], sib).wait_send()
    remote(wbuf.at[0], wbuf.at[0], s_ws.at[0], ws_r.at[0, 0], sib).wait_send()


def local_backward(act_blk, w_blk, grad_blk):
    any_spec = pl.BlockSpec(memory_space=pl.ANY)
    dma = pltpu.SemaphoreType.DMA
    outs = pl.pallas_call(
        kernel,
        out_shape=(
            jax.ShapeDtypeStruct((2048, 4096), BF16),
            jax.ShapeDtypeStruct((2048, 1024), F32),
            jax.ShapeDtypeStruct((2, 2, 2048, 1024), BF16),
            jax.ShapeDtypeStruct((3, 2, 4, 512, 256), F32),
            jax.ShapeDtypeStruct((2, 4, 512, 256), F32),
        ),
        in_specs=[any_spec] * 3,
        out_specs=(any_spec,) * 5,
        scratch_shapes=[
            pltpu.VMEM((2, 2, 2048, 1024), BF16),
            pltpu.VMEM((4, 2048, 512), BF16),
            pltpu.VMEM((4, 2048, 512), BF16),
            pltpu.VMEM((4, 4, 512, 256), F32),
            pltpu.VMEM((4, 4, 512, 256), F32),
            pltpu.VMEM((2, 2, 256, 1024), BF16),
            pltpu.VMEM((2, 2048, 256), BF16),
            pltpu.VMEM((4, 512, 256), F32),
            dma((5,)), dma((2, 4)), dma((4,)), dma((4,)), dma((2, 8)), dma((2, 8)), dma((24,)), dma((16,)),
            dma((1,)), dma((1,)), dma((1,)), dma((1,)), dma((1,)), dma((1,)), dma((1,)), dma((1,)),
            dma((2, 2)), dma((2,)), dma((4,)), dma((2,)),
        ],
        compiler_params=pltpu.CompilerParams(
            collective_id=0, has_side_effects=True, vmem_limit_bytes=66 * 1000 * 1000
        ),
        cost_estimate=pl.CostEstimate(flops=2 * 2048 * 2048 * 4096 * 2, bytes_accessed=100 << 20, transcendentals=0),
    )(act_blk, w_blk, grad_blk)
    return outs[0], outs[1]


def solution(mesh):
    io_spec = P(("dp", "row"), "col")
    w_spec = P("row", "col")
    return jax.shard_map(
        local_backward, mesh=mesh, in_specs=(io_spec, w_spec, io_spec), out_specs=(io_spec, io_spec), check_vma=False
    )
```

time: 1470 us -> 305 us (0.21)
  waiting for transfers between devices: 1350 us -> 0 us
  Pallas kernels: 0 us -> 285 us
  matrix products: 87.1 us -> 0 us
  local copies, waits for them, and re-layouts: 0 us -> 18 us
  other arithmetic: 17.4 us -> 0 us
    reduce_scatter x2 -> x0, waiting for transfers between devices: 897 us -> none  [the longest x1 686 us: local_backward(): lax.psum_scatter(grad_in_part, 'col', scatter_dimension=1, tiled=True)]
    all_gather x2 -> x0, waiting for transfers between devices: 450 us -> none  [the longest x1 342 us: local_backward(): act_rows = lax.all_gather(act_blk, 'col', axis=1, tiled=True)]
    pallas_call x0 -> x1, Pallas kernels: none -> 285 us  [local_backward(): pl.pallas_call(kernel, out_shape=(jax.ShapeDtypeStruct((2048, 4096), BF16...]
    dot_general x2 -> x0, matrix products: 87.1 us -> none  [the longest x1 45 us: local_backward(): jnp.einsum('tn,kn->tk', grad_blk, w_cols, preferred_element_type=jnp.floa...]
    unnamed x0 -> x4, local copies, waits for them, and re-layouts: none -> 18 us
    convert_element_type x1 -> x0, other arithmetic: 17.4 us -> none  [local_backward(): lax.psum_scatter(grad_in_part, 'col', scatter_dimension=1, tiled=True)]
  transfers between devices with their start and end apart: 4 -> 0, of which waited for: 4 -> 0; matrix products, arithmetic and copies ran while one was open for 7% -> 0% of each run, Pallas kernels for 0% -> 0%
where the time goes in v1:
time: 305 us; the launch traced here: 304 us
  Pallas kernels  285 us (93%)
  local copies, waits for them, and re-layouts  18 us (6%)
    pallas_call x1, Pallas kernels, local_backward(): pl.pallas_call(kernel, out_shape=(jax.ShapeDtypeStruct((2048, 4096), BF16...  285 us
    unnamed x4, local copies, waits for them, and re-layouts  18 us

profile of v1, /device:TPU:0, one launch (start us, length us, event | category | flops | bytes accessed | tf_op | source)
XLA Modules:
  0.0 303.7 jit_solution(113621926723476314)
XLA Ops:
  0.6 285.1 %shard_map.50 = (bf16[2048,4096]{1,0:T(8,128)(2,1)}, f32[2048,1024]{1,0:T(8,128)}, bf16[2,2,2048,1024]{3,2,1,0:T(8,128)(2,1)}, f32[3,2,4,512,256]{4,3,2,1,0:T(8,128)}, f32[2,4,512,256]{3,2,1,0:T(8,128)}) custom-call(bf16[2048,4096]{1,0:T(8,128)(2,1)} %x_ref.1, bf16[2048,1024]{1,0:T(8,128)(2,1)} %w_ref.1, bf16[2048,1024]{1,0:T(8,128)(2,1)} %dy_ref.1), custom_call_target="tpu_custom_call" | custom-call | flops 68719476736 | bytes 104857600 | tf_op jit(solution)/shard_map/pallas_call | solution.py:401
  285.7 0.0 copy-start
  285.7 14.6 %copy.7 = bf16[2048,4096]{1,0:T(8,128)(2,1)} copy(bf16[2048,4096]{1,0:T(8,128)(2,1)} %get-tuple-element.8) | data formatting | bytes 33554432
  300.3 0.0 copy-done
  300.3 3.4 %copy.8 = f32[2048,1024]{1,0:T(8,128)} copy(f32[2048,1024]{1,0:T(8,128)S(1)} %copy-done) | data formatting | bytes 16777216
Async XLA Ops:
  285.7 14.6 %copy-start = (f32[2048,1024]{1,0:T(8,128)S(1)}, f32[2048,1024]{1,0:T(8,128)}, u32[]{:S(2)}) copy-start(f32[2048,1024]{1,0:T(8,128)} %get-tuple-element.9) | copy-start | bytes 25165828

commit v2 on v1

--- a/solution.py
+++ b/solution.py
@@ -23,10 +23,10 @@
 def kernel(
     x_ref, w_ref, dy_ref,
     dx_ref, dw_ref, wbuf, bufx, bufy,
-    dyv, xo, xs, pown, poth, wv, xv, lb,
+    dyv, pown, poth, wv, lb,
     ld_sem, dys_r, dyy_r, xs_r, w_r, ws_r, px_r, py_r,
     s_dys, s_dyy, s_xs, s_w, s_ws, s_px, s_py, s_sum,
-    wl_sem, xv_sem, lb_sem, out_sem,
+    wl_sem, lb_sem,
 ):
     row = lax.axis_index("row")
     y = lax.axis_index("col")
@@ -37,6 +37,7 @@
     sib = {"row": row + 1 - 2 * c}
     xn = {"row": (row + 2) % 4}
     yn = {"col": 1 - y}
+    diag = {"row": (row + 2) % 4, "col": 1 - y}
 
     def remote(src, dst, ssem, rsem, dev):
         return pltpu.make_async_remote_copy(
@@ -50,9 +51,18 @@
         return pl.ds(q * 256, 256)
 
     barrier = pltpu.get_barrier_semaphore()
-    for dev in (sib, xn, yn):
+    for dev in (sib, xn, yn, diag):
         pl.semaphore_signal(barrier, inc=1, device_id=dev, device_id_type=MESH)
-    pl.semaphore_wait(barrier, 3)
+    pl.semaphore_wait(barrier, 4)
+
+    def xo(kt):
+        return dx_ref.at[:, pl.ds(pl.multiple_of(kt * 512, 512), 512)]
+
+    def xs(kt):
+        return dx_ref.at[:, pl.ds(pl.multiple_of(2048 + kt * 512, 512), 512)]
+
+    def dw_tile(q, kt):
+        return dw_ref.at[pl.ds(kt * 512, 512), pl.ds(pl.multiple_of(q * 256, 256), 256)]
 
     def dy_to_sib(j, q):
         src = dy_ref.at[:, qs(q)] if j == 0 else dyv.at[0, 1, :, qs(q)]
@@ -62,11 +72,11 @@
         return remote(dy_ref.at[:, qs(q)], dyv.at[0, 1, :, qs(q)], s_dyy.at[0], dyy_r.at[q], yn)
 
     def x_load(kt):
-        return local(x_ref.at[:, pl.ds(c * 2048 + kt * 512, 512)], xo.at[kt], ld_sem.at[1 + kt])
+        return local(x_ref.at[:, pl.ds(c * 2048 + kt * 512, 512)], xo(kt), ld_sem.at[1 + kt])
 
     def x_to_sib(kt):
         return remote(
-            x_ref.at[:, pl.ds((1 - c) * 2048 + kt * 512, 512)], xs.at[kt], s_xs.at[0], xs_r.at[kt], sib
+            x_ref.at[:, pl.ds((1 - c) * 2048 + kt * 512, 512)], xs(kt), s_xs.at[0], xs_r.at[kt], sib
         )
 
     def rows(i):
@@ -88,24 +98,17 @@
     def p_to_x(g, src, q, kt):
         return remote(src.at[q, kt], bufx.at[g, q % 2, kt], s_px.at[0], px_r.at[g * 8 + (q % 2) * 4 + kt], xn)
 
-    def p_to_y_half(q, kt, h):
-        part = pl.ds(h * 256, 256)
-        return remote(
-            poth.at[q, kt, part], bufy.at[q, kt, part], s_py.at[0], py_r.at[q * 8 + kt * 2 + h], yn
-        )
-
-    def p_fwd(i):
+    def p_diag(i):
         q, kt, h = i // 8, (i // 2) % 4, i % 2
         part = pl.ds(h * 256, 256)
-        return remote(bufy.at[q, kt, part], bufx.at[0, q, kt, part], s_px.at[0], px_r.at[i], xn)
+        return remote(poth.at[q, kt, part], bufx.at[0, q, kt, part], s_py.at[0], px_r.at[i], diag)
 
     def p_term(q, kt):
         return remote(poth.at[q, kt], bufy.at[q, kt], s_py.at[0], py_r.at[q * 4 + kt], yn)
 
     def sum_to_y(q, kt):
         return remote(
-            poth.at[q, kt], dw_ref.at[pl.ds(kt * 512, 512), qs(q)], s_sum.at[0],
-            py_r.at[8 + (q - 2) * 4 + kt], yn,
+            poth.at[q, kt], dw_tile(q, kt), s_sum.at[0], py_r.at[8 + (q - 2) * 4 + kt], yn
         )
 
     dy_load = local(dy_ref, dyv.at[0, 0], ld_sem.at[0])
@@ -144,8 +147,8 @@
             w_to_sib(0, i, True).start()
 
     def p_tile(dst, j, q, kt):
-        dst[q, kt] = _tdot(xo[kt], dyv[0, j, :, q * 256:(q + 1) * 256]) + _tdot(
-            xs[kt], dyv[1, j, :, q * 256:(q + 1) * 256]
+        dst[q, kt] = _tdot(xo(kt)[...], dyv[0, j, :, q * 256:(q + 1) * 256]) + _tdot(
+            xs(kt)[...], dyv[1, j, :, q * 256:(q + 1) * 256]
         )
 
     dy_load.wait()
@@ -179,8 +182,8 @@
 
                 @pl.when(is_b)
                 def _():
-                    p_to_y_half(q, kt, 0).start()
-                    p_to_y_half(q, kt, 1).start()
+                    p_diag(8 * q + 2 * kt).start()
+                    p_diag(8 * q + 2 * kt + 1).start()
             else:
                 @pl.when(is_b)
                 def _():
@@ -196,8 +199,7 @@
         ld = local(bufx.at[g, q2, kt], lb.at[0], lb_sem.at[0])
         ld.start()
         ld.wait()
-        pown[q, kt] = pown[q, kt] + lb[0]
-        local(pown.at[q, kt], dw_ref.at[pl.ds(kt * 512, 512), qs(q)], out_sem.at[0]).start()
+        dw_tile(q, kt)[...] = pown[q, kt] + lb[0]
 
     def a_sum(q, kt):
         p_to_x(1, poth, q, kt).wait_recv()
@@ -221,24 +223,18 @@
             first = local(wbuf.at[cc, 0, rows(d)], wv.at[slot, 0], wl_sem.at[slot, 0])
         return first, local(wbuf.at[cc, 1, rows(d)], wv.at[slot, 1], wl_sem.at[slot, 1])
 
-    def xv_out(d, cc):
+    def dx_stripe(d, cc):
         k0 = (c + cc * (1 - 2 * c)) * 2048
-        return local(xv.at[cc], dx_ref.at[:, pl.ds(k0 + d * 256, 256)], xv_sem.at[cc])
-
-    def dx_stripe(d, cc):
-        @pl.when(d > 0)
-        def _():
-            xv_out(d, cc).wait()
+        cols = pl.ds(pl.multiple_of(k0 + d * 256, 256), 256)
 
         def body(m, carry):
             part = pl.ds(m * 512, 512)
-            xv[cc, part, :] = (
+            dx_ref[part, cols] = (
                 _dot_t(dyv[0, 0, part, :], wv[cc, 0]) + _dot_t(dyv[0, 1, part, :], wv[cc, 1])
             ).astype(BF16)
             return carry
 
         lax.fori_loop(0, 4, body, 0)
-        xv_out(d, cc).start()
 
     def start_loads(d, cc, own_from_arg):
         for cp in w_loads(2 * d + cc, own_from_arg):
@@ -284,8 +280,6 @@
         start_loads(0, 0, True)
 
         def body(d, carry):
-            p_to_y_half(d // 4, d % 4, 0).wait_recv()
-            p_fwd(2 * d).start()
             sib_wait(d)
             start_loads(d, 1, False)
             wait_loads(d, 0, True)
@@ -295,9 +289,6 @@
             def _():
                 a_sum(3, d)
 
-            p_to_y_half(d // 4, d % 4, 1).wait_recv()
-            p_fwd(2 * d + 1).start()
-
             @pl.when(d < 7)
             def _():
                 start_loads(d + 1, 0, True)
@@ -313,11 +304,7 @@
         lax.fori_loop(0, 8, body, 0)
         a_final(2, 6)
         a_final(2, 7)
-        for cc in range(2):
-            xv_out(7, cc).wait()
-        local(dw_ref, dw_ref, out_sem.at[0]).wait()
         remote(wbuf.at[0], wbuf.at[0], s_w.at[0], w_r.at[0, 0], xn).wait_send()
-        remote(bufx.at[0], bufx.at[0], s_px.at[0], px_r.at[0], xn).wait_send()
         remote(bufy, bufy, s_py.at[0], py_r.at[0], yn).wait_send()
         remote(bufy, bufy, s_sum.at[0], py_r.at[0], yn).wait_send()
 
@@ -349,13 +336,6 @@
 
         lax.fori_loop(0, 8, body, 0)
 
-        def out_half(q, kt, h, slot):
-            return local(
-                lb.at[2 + slot, pl.ds(0, 256)],
-                dw_ref.at[pl.ds(kt * 512 + h * 256, 256), pl.ds(q * 256, 256)],
-                out_sem.at[slot],
-            )
-
         def fin(i, carry):
             q, kt = i // 4, i % 4
             p_term(q, kt).wait_recv()
@@ -363,71 +343,81 @@
                 part = pl.ds(h * 256, 256)
                 first = local(bufy.at[q, kt, part], lb.at[h, pl.ds(0, 256)], lb_sem.at[h])
                 first.start()
-                p_fwd(i * 2 + h).wait_recv()
+                p_diag(i * 2 + h).wait_recv()
                 second = local(bufx.at[0, q, kt, part], lb.at[h, pl.ds(256, 256)], lb_sem.at[2 + h])
                 second.start()
-
-                @pl.when(i > 0)
-                def _():
-                    out_half(q, kt, h, h).wait()
-
                 first.wait()
                 second.wait()
-                lb[2 + h, 0:256] = lb[h, 0:256] + lb[h, 256:512]
-                out_half(q, kt, h, h).start()
+                dw_ref[pl.ds(kt * 512 + h * 256, 256), pl.ds(pl.multiple_of(q * 256, 256), 256)] = (
+                    lb[h, 0:256] + lb[h, 256:512]
+                )
             return carry
 
         lax.fori_loop(0, 8, fin, 0)
         for q in range(2, 4):
             for kt in range(4):
                 sum_to_y(q, kt).wait_recv()
-        for h in range(2):
-            out_half(1, 3, h, h).wait()
-        for cc in range(2):
-            xv_out(7, cc).wait()
         remote(wbuf.at[0, 0], wbuf.at[0, 0], s_w.at[0], w_r.at[0, 0], yn).wait_send()
         remote(bufx, bufx, s_px.at[0], px_r.at[0], xn).wait_send()
         remote(bufy, bufy, s_py.at[0], py_r.at[0], yn).wait_send()
 
     remote(dyv.at[0], dyv.at[0], s_dys.at[0], dys_r.at[0, 0], sib).wait_send()
     remote(dyv.at[0, 0], dyv.at[0, 0], s_dyy.at[0], dyy_r.at[0], yn).wait_send()
-    remote(xs, xs, s_xs.at[0], xs_r.at[0], sib).wait_send()
+    remote(wbuf.at[0], wbuf.at[0], s_xs.at[0], xs_r.at[0], sib).wait_send()
     remote(wbuf.at[0], wbuf.at[0], s_ws.at[0], ws_r.at[0, 0], sib).wait_send()
+
+
+def store_kernel(dx_ref, dw_ref, dx_out, dw_out, sem):
+    copies = []
+    for i in range(4):
+        part = pl.ds(i * 512, 512)
+        copies.append(pltpu.make_async_copy(dx_ref.at[part], dx_out.at[part], sem.at[2 * i]))
+        copies.append(pltpu.make_async_copy(dw_ref.at[part], dw_out.at[part], sem.at[2 * i + 1]))
+    for cp in copies:
+        cp.start()
+    for cp in copies:
+        cp.wait()
 
 
 def local_backward(act_blk, w_blk, grad_blk):
     any_spec = pl.BlockSpec(memory_space=pl.ANY)
+    vmem_spec = pl.BlockSpec(memory_space=pltpu.VMEM)
     dma = pltpu.SemaphoreType.DMA
     outs = pl.pallas_call(
         kernel,
         out_shape=(
-            jax.ShapeDtypeStruct((2048, 4096), BF16),
-            jax.ShapeDtypeStruct((2048, 1024), F32),
+            pltpu.VMEM((2048, 4096), BF16),
+            pltpu.VMEM((2048, 1024), F32),
             jax.ShapeDtypeStruct((2, 2, 2048, 1024), BF16),
             jax.ShapeDtypeStruct((3, 2, 4, 512, 256), F32),
             jax.ShapeDtypeStruct((2, 4, 512, 256), F32),
         ),
         in_specs=[any_spec] * 3,
-        out_specs=(any_spec,) * 5,
+        out_specs=(vmem_spec, vmem_spec) + (any_spec,) * 3,
         scratch_shapes=[
             pltpu.VMEM((2, 2, 2048, 1024), BF16),
-            pltpu.VMEM((4, 2048, 512), BF16),
-            pltpu.VMEM((4, 2048, 512), BF16),
             pltpu.VMEM((4, 4, 512, 256), F32),
             pltpu.VMEM((4, 4, 512, 256), F32),
             pltpu.VMEM((2, 2, 256, 1024), BF16),
-            pltpu.VMEM((2, 2048, 256), BF16),
-            pltpu.VMEM((4, 512, 256), F32),
+            pltpu.VMEM((2, 512, 256), F32),
             dma((5,)), dma((2, 4)), dma((4,)), dma((4,)), dma((2, 8)), dma((2, 8)), dma((24,)), dma((16,)),
             dma((1,)), dma((1,)), dma((1,)), dma((1,)), dma((1,)), dma((1,)), dma((1,)), dma((1,)),
-            dma((2, 2)), dma((2,)), dma((4,)), dma((2,)),
+            dma((2, 2)), dma((4,)),
         ],
         compiler_params=pltpu.CompilerParams(
-            collective_id=0, has_side_effects=True, vmem_limit_bytes=66 * 1000 * 1000
+            collective_id=0, has_side_effects=True, vmem_limit_bytes=39 << 20
         ),
         cost_estimate=pl.CostEstimate(flops=2 * 2048 * 2048 * 4096 * 2, bytes_accessed=100 << 20, transcendentals=0),
     )(act_blk, w_blk, grad_blk)
-    return outs[0], outs[1]
+    return pl.pallas_call(
+        store_kernel,
+        out_shape=(jax.ShapeDtypeStruct((2048, 4096), BF16), jax.ShapeDtypeStruct((2048, 1024), F32)),
+        in_specs=[vmem_spec, vmem_spec],
+        out_specs=(any_spec, any_spec),
+        scratch_shapes=[dma((8,))],
+        compiler_params=pltpu.CompilerParams(vmem_limit_bytes=1 << 20),
+        cost_estimate=pl.CostEstimate(flops=0, bytes_accessed=48 << 20, transcendentals=0),
+    )(outs[0], outs[1])
 
 
 def solution(mesh):

time: 305 us -> 385 us (1.26)
  Pallas kernels: 285 us -> 383 us
  local copies, waits for them, and re-layouts: 18 us -> 0 us
    pallas_call x1 -> x2, Pallas kernels: 285 us -> 383 us  [the longest x1 374 us: local_backward(): pl.pallas_call(kernel, out_shape=(pltpu.VMEM((2048, 4096), BF16), pltpu.V...]
    unnamed x4 -> x0, local copies, waits for them, and re-layouts: 18 us -> none
where the time goes in v2:
time: 385 us; the launch traced here: 383 us
  Pallas kernels  383 us (99%)
    pallas_call x1, Pallas kernels, local_backward(): pl.pallas_call(kernel, out_shape=(pltpu.VMEM((2048, 4096), BF16), pltpu.V...  374 us
    pallas_call x1, Pallas kernels, local_backward(): pl.pallas_call(store_kernel, out_shape=(jax.ShapeDtypeStruct((2048, 4096)...  8.45 us

profile of v2, /device:TPU:0, one launch (start us, length us, event | category | flops | bytes accessed | tf_op | source)
XLA Modules:
  0.0 383.4 jit_solution(17838916837962495491)
XLA Ops:
  0.6 374.1 %shard_map.50 = (bf16[2048,4096]{1,0:T(8,128)(2,1)S(1)}, f32[2048,1024]{1,0:T(8,128)S(1)}, bf16[2,2,2048,1024]{3,2,1,0:T(8,128)(2,1)}, f32[3,2,4,512,256]{4,3,2,1,0:T(8,128)}, f32[2,4,512,256]{3,2,1,0:T(8,128)}) custom-call(bf16[2048,4096]{1,0:T(8,128)(2,1)} %x_ref.1, bf16[2048,1024]{1,0:T(8,128)(2,1)} %w_ref.1, bf16[2048,1024]{1,0:T(8,128)(2,1)} %dy_ref.1), custom_call_target="tpu_custom_call" | custom-call | flops 68719476736 | bytes 104857600 | tf_op jit(solution)/shard_map/pallas_call | solution.py:386
  374.8 8.4 %shard_map.51 = (bf16[2048,4096]{1,0:T(8,128)(2,1)}, f32[2048,1024]{1,0:T(8,128)}) custom-call(bf16[2048,4096]{1,0:T(8,128)(2,1)S(1)} %get-tuple-element.4.dx_ref, f32[2048,1024]{1,0:T(8,128)S(1)} %get-tuple-element.5.dw_ref), custom_call_target="tpu_custom_call" | custom-call | bytes 50331648 | tf_op jit(solution)/shard_map/pallas_call | solution.py:412

commit v3 on v2

v3 whole, which is shorter than its diff:
```python
import functools

import jax
import jax.numpy as jnp
from jax import lax
from jax.experimental import pallas as pl
from jax.experimental.pallas import tpu as pltpu
from jax.sharding import PartitionSpec as P

MESH = pl.DeviceIdType.MESH
F32 = jnp.float32
BF16 = jnp.bfloat16


def _tdot(a, b):
    return lax.dot_general(a, b, (((0,), (0,)), ((), ())), preferred_element_type=F32)


def _dot_t(a, b):
    return lax.dot_general(a, b, (((1,), (1,)), ((), ())), preferred_element_type=F32)


def kernel(
    x_ref, w_ref, dy_ref,
    dx_ref, dw_ref, wbuf, bufy,
    dyv, pown, poth, wv, land,
    ld_sem, dys_r, dyy_r, xs_r, w_r, ws_r, px_r, py_r, pf_r,
    s_dys, s_dyy, s_xs, s_w, s_ws, s_px, s_py, s_sum, wl_sem,
):
    row = lax.axis_index("row")
    y = lax.axis_index("col")
    x = row // 2
    c = row % 2
    is_a = x == y
    is_b = x != y
    sib = {"row": row + 1 - 2 * c}
    xn = {"row": (row + 2) % 4}
    yn = {"col": 1 - y}

    def remote(src, dst, ssem, rsem, dev):
        return pltpu.make_async_remote_copy(
            src_ref=src, dst_ref=dst, send_sem=ssem, recv_sem=rsem, device_id=dev, device_id_type=MESH
        )

    def local(src, dst, sem):
        return pltpu.make_async_copy(src, dst, sem)

    def qs(q):
        return pl.ds(q * 256, 256)

    def xo(k0, n):
        return dx_ref.at[:, pl.ds(pl.multiple_of(k0, 256), n)]

    def xs(k0, n):
        return dx_ref.at[:, pl.ds(pl.multiple_of(2048 + k0, 256), n)]

    def dw_tile(q, kt, r0=0, n=512):
        return dw_ref.at[pl.ds(kt * 512 + r0, n), pl.ds(pl.multiple_of(q * 256, 256), 256)]

    dy_load = local(dy_ref, dyv.at[0, 0], ld_sem.at[0])

    def x_load(kt):
        return local(x_ref.at[:, pl.ds(c * 2048 + kt * 512, 512)], xo(kt * 512, 512), ld_sem.at[1 + kt])

    def x_to_sib(kt):
        return remote(
            x_ref.at[:, pl.ds((1 - c) * 2048 + kt * 512, 512)], xs(kt * 512, 512), s_xs.at[0], xs_r.at[1 + kt], sib
        )

    def x_to_sib_half(h):
        return remote(
            x_ref.at[:, pl.ds((1 - c) * 2048 + h * 256, 256)], xs(h * 256, 256), s_xs.at[0], xs_r.at[h], sib
        )

    def dy_to_sib(j, q):
        src = dy_ref.at[:, qs(q)] if j == 0 else dyv.at[0, 1, :, qs(q)]
        return remote(src, dyv.at[1, j, :, qs(q)], s_dys.at[0], dys_r.at[j, q], sib)

    def dy_to_y(q):
        return remote(dy_ref.at[:, qs(q)], dyv.at[0, 1, :, qs(q)], s_dyy.at[0], dyy_r.at[q], yn)

    def rows(i):
        return pl.ds(i * 256, 256)

    def w_own_to_x(i):
        return remote(w_ref.at[rows(i)], wbuf.at[0, 0, rows(i)], s_w.at[0], w_r.at[0, i], xn)

    def w_to_y(i):
        return remote(w_ref.at[rows(i)], wbuf.at[0, 1, rows(i)], s_w.at[0], w_r.at[1, i], yn)

    def w_fwd(i):
        return remote(wbuf.at[0, 1, rows(i)], wbuf.at[0, 1, rows(i)], s_w.at[0], w_r.at[1, i], xn)

    def w_to_sib(j, i, own):
        src = w_ref.at[rows(i)] if own else wbuf.at[0, j, rows(i)]
        return remote(src, wbuf.at[1, j, rows(i)], s_ws.at[0], ws_r.at[j, i], sib)

    def p_own_half(q, kt, h):
        return remote(
            pown.at[q, kt, pl.ds(h * 256, 256)], dw_tile(q, kt, h * 256, 256), s_px.at[0],
            px_r.at[q * 8 + kt * 2 + h], xn,
        )

    def p_own(q, kt):
        return remote(pown.at[q, kt], dw_tile(q, kt), s_px.at[0], px_r.at[16 + (q - 2) * 4 + kt], xn)

    def p_other(q, kt):
        return remote(poth.at[q, kt], land.at[q - 2, kt], s_px.at[1], px_r.at[24 + (q - 2) * 4 + kt], xn)

    def p_trans(i):
        q, kt, r = i // 16, (i // 4) % 4, i % 4
        part = pl.ds(r * 128, 128)
        return remote(poth.at[q, kt, part], bufy.at[q, kt, part], s_py.at[0], pf_r.at[i], yn)

    def p_fwd(i):
        q, kt, r = i // 16, (i // 4) % 4, i % 4
        part = pl.ds(r * 128, 128)
        return remote(bufy.at[q, kt, part], land.at[q, kt, part], s_px.at[0], pf_r.at[i], xn)

    def p_term(q, kt):
        return remote(poth.at[q, kt], dw_tile(q, kt), s_py.at[0], py_r.at[q * 4 + kt], yn)

    def sum_to_y(q, kt):
        return remote(poth.at[q, kt], dw_tile(q, kt), s_sum.at[0], py_r.at[q * 4 + kt], yn)

    dy_load.start()
    for kt in range(4):
        x_load(kt).start()

    barrier = pltpu.get_barrier_semaphore()
    for dev in (sib, xn, yn):
        pl.semaphore_signal(barrier, inc=1, device_id=dev, device_id_type=MESH)
    pl.semaphore_wait(barrier, 3)

    dy_to_sib(0, 0).start()
    x_to_sib_half(0).start()
    dy_to_y(0).start()
    dy_to_y(1).start()

    @pl.when(is_a)
    def _():
        for i in range(8):
            w_own_to_x(i).start()
        for q in range(2, 4):
            dy_to_y(q).start()

    @pl.when(is_b)
    def _():
        for i in range(8):
            w_to_y(i).start()
        dy_to_y(2).start()

    x_to_sib_half(1).start()
    for kt in range(1, 4):
        x_to_sib(kt).start()
    for q in range(1, 4):
        dy_to_sib(0, q).start()

    @pl.when(is_a)
    def _():
        for i in range(8):
            w_to_sib(0, i, True).start()

    def p_part(j, q, k0, n):
        return _tdot(xo(k0, n)[...], dyv[0, j, :, q * 256:(q + 1) * 256]) + _tdot(
            xs(k0, n)[...], dyv[1, j, :, q * 256:(q + 1) * 256]
        )

    dy_load.wait()
    for q in range(4):
        dy_to_sib(0, q).wait_recv()
        if q == 0:
            x_load(0).wait()
            for h in range(2):
                x_to_sib_half(h).wait_recv()
                pown[0, 0, h * 256:(h + 1) * 256] = p_part(0, 0, h * 256, 256)

                @pl.when(is_b)
                def _(h=h):
                    p_own_half(0, 0, h).start()

        def own_body(kt, carry, q=q):
            if q == 0:
                x_load(kt).wait()
                x_to_sib(kt).wait_recv()
            for h in range(2):
                pown[q, kt, h * 256:(h + 1) * 256] = p_part(0, q, kt * 512 + h * 256, 256)
            if q < 2:
                @pl.when(is_b)
                def _():
                    p_own_half(q, kt, 0).start()
                    p_own_half(q, kt, 1).start()
            return carry

        lax.fori_loop(1 if q == 0 else 0, 4, own_body, 0)

    def other_tile(q, kt):
        for h in range(2):
            poth[q, kt, h * 256:(h + 1) * 256] = p_part(1, q, kt * 512 + h * 256, 256)

    def trans_tile(q, kt):
        for r in range(4):
            p_trans(16 * q + 4 * kt + r).start()

    def dy_in(q):
        dy_to_y(q).wait_recv()
        dy_to_sib(1, q).start()

    def other_pass(q):
        dy_in(q)
        dy_to_sib(1, q).wait_recv()

        def body(kt, carry):
            other_tile(q, kt)
            if q < 2:
                @pl.when(is_a)
                def _():
                    p_term(q, kt).start()

                @pl.when(is_b)
                def _():
                    trans_tile(q, kt)
                    if q == 0:
                        @pl.when(kt == 0)
                        def _():
                            dy_to_y(3).start()
            else:
                @pl.when(is_b)
                def _():
                    p_other(q, kt).start()
            return carry

        lax.fori_loop(0, 4, body, 0)

    def w_loads(d, cc, own_from_arg):
        if own_from_arg:
            first = local(w_ref.at[rows(d)], wv.at[cc, 0], wl_sem.at[cc, 0])
        else:
            first = local(wbuf.at[cc, 0, rows(d)], wv.at[cc, 0], wl_sem.at[cc, 0])
        return first, local(wbuf.at[cc, 1, rows(d)], wv.at[cc, 1], wl_sem.at[cc, 1])

    def start_loads(d, cc, own_from_arg):
        for cp in w_loads(d, cc, own_from_arg):
            cp.start()

    def wait_loads(d, cc, own_from_arg):
        for cp in w_loads(d, cc, own_from_arg):
            cp.wait()

    def dx_stripe(d, cc):
        k0 = (c + cc * (1 - 2 * c)) * 2048
        cols = pl.ds(pl.multiple_of(k0 + d * 256, 256), 256)

        def body(m, carry):
            part = pl.ds(m * 512, 512)
            dx_ref[part, cols] = (
                _dot_t(dyv[0, 0, part, :], wv[cc, 0]) + _dot_t(dyv[0, 1, part, :], wv[cc, 1])
            ).astype(BF16)
            return carry

        lax.fori_loop(0, 4, body, 0)

    def pair_wait(d, own_from_arg):
        w_to_sib(0, d, own_from_arg).wait_recv()
        w_to_sib(1, d, False).wait_recv()

    other_pass(0)
    other_pass(1)

    @pl.when(is_a)
    def _():
        def add(q, kt):
            tile = dw_tile(q, kt)
            tile[...] = tile[...] + pown[q, kt]

        def final_early(t):
            q, kt = t // 4, t % 4
            for h in range(2):
                p_own_half(q, kt, h).wait_recv()
            add(q, kt)

        def final_late(t):
            q, kt = 2 + t // 4, t % 4
            p_own(q, kt).wait_recv()
            add(q, kt)

        def a_sum(q, kt):
            p_other(q, kt).wait_recv()
            poth[q, kt] = poth[q, kt] + land[q - 2, kt]
            sum_to_y(q, kt).start()

        def fwd(i):
            p_trans(i).wait_recv()
            p_fwd(i).start()

        def early(i, carry):
            w_to_y(i).wait_recv()
            w_fwd(i).start()
            w_to_sib(1, i, False).start()
            final_early(i)
            return carry

        lax.fori_loop(0, 8, early, 0)

        dy_in(2)
        dy_to_sib(1, 2).wait_recv()

        def q2_body(kt, carry):
            other_tile(2, kt)
            a_sum(2, kt)
            fwd(kt)
            return carry

        lax.fori_loop(0, 4, q2_body, 0)

        pair_wait(0, True)
        start_loads(0, 0, True)
        dy_in(3)
        fwd(4)
        dy_to_sib(1, 3).wait_recv()

        def q3_body(kt, carry):
            other_tile(3, kt)

            @pl.when(kt < 3)
            def _():
                fwd(5 + kt)
            return carry

        lax.fori_loop(0, 4, q3_body, 0)

        def late(d, carry):
            @pl.when(d < 6)
            def _():
                fwd(4 * d + 8)
            start_loads(d, 1, False)
            wait_loads(d, 0, True)
            dx_stripe(d, 0)

            @pl.when(d < 6)
            def _():
                fwd(4 * d + 9)

            @pl.when(d < 7)
            def _():
                pair_wait(d + 1, True)
                start_loads(d + 1, 0, True)

            @pl.when(d < 4)
            def _():
                a_sum(3, d)

            @pl.when(d < 6)
            def _():
                fwd(4 * d + 10)
            wait_loads(d, 1, False)
            dx_stripe(d, 1)

            @pl.when(d < 6)
            def _():
                fwd(4 * d + 11)
                final_late(d)
            return carry

        lax.fori_loop(0, 8, late, 0)
        final_late(6)
        final_late(7)
        remote(wbuf.at[0], wbuf.at[0], s_w.at[0], w_r.at[0, 0], xn).wait_send()
        remote(land, land, s_px.at[0], px_r.at[0], xn).wait_send()
        remote(land, land, s_py.at[0], py_r.at[0], yn).wait_send()
        remote(land, land, s_sum.at[0], py_r.at[0], yn).wait_send()

    @pl.when(is_b)
    def _():
        other_pass(2)
        other_pass(3)
        for q in range(2, 4):
            for kt in range(4):
                p_own(q, kt).start()

        def own_w(i, carry):
            w_own_to_x(i).wait_recv()
            w_to_sib(0, i, False).start()
            return carry

        lax.fori_loop(0, 8, own_w, 0)

        def stripes(d, carry):
            w_to_y(d).wait_recv()
            w_to_sib(1, d, False).start()
            start_loads(d, 0, False)
            pair_wait(d, False)
            start_loads(d, 1, False)
            wait_loads(d, 0, False)
            dx_stripe(d, 0)
            wait_loads(d, 1, False)
            dx_stripe(d, 1)
            return carry

        lax.fori_loop(0, 8, stripes, 0)

        def fin(i, carry):
            q, kt, r = i // 16, (i // 4) % 4, i % 4

            @pl.when(r == 0)
            def _():
                p_term(q, kt).wait_recv()
            p_fwd(i).wait_recv()
            tile = dw_tile(q, kt, r * 128, 128)
            tile[...] = tile[...] + land[q, kt, pl.ds(r * 128, 128)]
            return carry

        lax.fori_loop(0, 32, fin, 0)
        for q in range(2, 4):
            for kt in range(4):
                sum_to_y(q, kt).wait_recv()
        remote(wbuf.at[0, 0], wbuf.at[0, 0], s_w.at[0], w_r.at[0, 0], yn).wait_send()
        remote(pown, pown, s_px.at[0], px_r.at[0], xn).wait_send()
        remote(land, land, s_px.at[1], px_r.at[0], xn).wait_send()
        remote(land, land, s_py.at[0], py_r.at[0], yn).wait_send()

    remote(dyv.at[0], dyv.at[0], s_dys.at[0], dys_r.at[0, 0], sib).wait_send()
    remote(dyv.at[0, 0], dyv.at[0, 0], s_dyy.at[0], dyy_r.at[0], yn).wait_send()
    remote(wbuf.at[0], wbuf.at[0], s_xs.at[0], xs_r.at[0], sib).wait_send()
    remote(wbuf.at[0], wbuf.at[0], s_ws.at[0], ws_r.at[0, 0], sib).wait_send()


def store_kernel(dx_ref, dw_ref, dx_out, dw_out, sem):
    copies = []
    for i in range(4):
        part = pl.ds(i * 512, 512)
        copies.append(pltpu.make_async_copy(dx_ref.at[part], dx_out.at[part], sem.at[2 * i]))
        copies.append(pltpu.make_async_copy(dw_ref.at[part], dw_out.at[part], sem.at[2 * i + 1]))
    for cp in copies:
        cp.start()
    for cp in copies:
        cp.wait()


def local_backward(act_blk, w_blk, grad_blk):
    any_spec = pl.BlockSpec(memory_space=pl.ANY)
    vmem_spec = pl.BlockSpec(memory_space=pltpu.VMEM)
    dma = pltpu.SemaphoreType.DMA
    outs = pl.pallas_call(
        kernel,
        out_shape=(
            pltpu.VMEM((2048, 4096), BF16),
            pltpu.VMEM((2048, 1024), F32),
            jax.ShapeDtypeStruct((2, 2, 2048, 1024), BF16),
            jax.ShapeDtypeStruct((2, 4, 512, 256), F32),
        ),
        in_specs=[any_spec] * 3,
        out_specs=(vmem_spec, vmem_spec) + (any_spec,) * 2,
        scratch_shapes=[
            pltpu.VMEM((2, 2, 2048, 1024), BF16),
            pltpu.VMEM((4, 4, 512, 256), F32),
            pltpu.VMEM((4, 4, 512, 256), F32),
            pltpu.VMEM((2, 2, 256, 1024), BF16),
            pltpu.VMEM((2, 4, 512, 256), F32),
            dma((5,)), dma((2, 4)), dma((4,)), dma((5,)), dma((2, 8)), dma((2, 8)), dma((32,)), dma((16,)), dma((32,)),
            dma((1,)), dma((1,)), dma((1,)), dma((1,)), dma((1,)), dma((2,)), dma((1,)), dma((1,)), dma((2, 2)),
        ],
        compiler_params=pltpu.CompilerParams(
            collective_id=0, has_side_effects=True, vmem_limit_bytes=41_800_000
        ),
        cost_estimate=pl.CostEstimate(flops=2 * 2048 * 2048 * 4096 * 2, bytes_accessed=100 << 20, transcendentals=0),
    )(act_blk, w_blk, grad_blk)
    return pl.pallas_call(
        store_kernel,
        out_shape=(jax.ShapeDtypeStruct((2048, 4096), BF16), jax.ShapeDtypeStruct((2048, 1024), F32)),
        in_specs=[vmem_spec, vmem_spec],
        out_specs=(any_spec, any_spec),
        scratch_shapes=[dma((8,))],
        compiler_params=pltpu.CompilerParams(vmem_limit_bytes=1 << 20),
        cost_estimate=pl.CostEstimate(flops=0, bytes_accessed=48 << 20, transcendentals=0),
    )(outs[0], outs[1])


def solution(mesh):
    io_spec = P(("dp", "row"), "col")
    w_spec = P("row", "col")
    return jax.shard_map(
        local_backward, mesh=mesh, in_specs=(io_spec, w_spec, io_spec), out_specs=(io_spec, io_spec), check_vma=False
    )
```

time: 385 us -> 300 us (0.78)
  Pallas kernels: 383 us -> 299 us
    pallas_call x1, Pallas kernels: 374 us -> 290 us  [local_backward(): pl.pallas_call(kernel, out_shape=(pltpu.VMEM((2048, 4096), BF16), pltpu.V...]
where the time goes in v3:
time: 300 us; the launch traced here: 299 us
  Pallas kernels  299 us (100%)
    pallas_call x1, Pallas kernels, local_backward(): pl.pallas_call(kernel, out_shape=(pltpu.VMEM((2048, 4096), BF16), pltpu.V...  290 us
    pallas_call x1, Pallas kernels, local_backward(): pl.pallas_call(store_kernel, out_shape=(jax.ShapeDtypeStruct((2048, 4096)...  8.45 us

profile of v3, /device:TPU:0, one launch (start us, length us, event | category | flops | bytes accessed | tf_op | source)
XLA Modules:
  0.0 299.4 jit_solution(2517053713751124874)
XLA Ops:
  0.6 290.2 %shard_map.50 = (bf16[2048,4096]{1,0:T(8,128)(2,1)S(1)}, f32[2048,1024]{1,0:T(8,128)S(1)}, bf16[2,2,2048,1024]{3,2,1,0:T(8,128)(2,1)}, f32[2,4,512,256]{3,2,1,0:T(8,128)}) custom-call(bf16[2048,4096]{1,0:T(8,128)(2,1)} %x_ref.1, bf16[2048,1024]{1,0:T(8,128)(2,1)} %w_ref.1, bf16[2048,1024]{1,0:T(8,128)(2,1)} %dy_ref.1), custom_call_target="tpu_custom_call" | custom-call | flops 68719476736 | bytes 104857600 | tf_op jit(solution)/shard_map/pallas_call | solution.py:444
  290.8 8.4 %shard_map.51 = (bf16[2048,4096]{1,0:T(8,128)(2,1)}, f32[2048,1024]{1,0:T(8,128)}) custom-call(bf16[2048,4096]{1,0:T(8,128)(2,1)S(1)} %get-tuple-element.4.dx_ref, f32[2048,1024]{1,0:T(8,128)S(1)} %get-tuple-element.5.dw_ref), custom_call_target="tpu_custom_call" | custom-call | bytes 50331648 | tf_op jit(solution)/shard_map/pallas_call | solution.py:468

commit v4 on v3

--- a/solution.py
+++ b/solution.py
@@ -24,7 +24,7 @@
     x_ref, w_ref, dy_ref,
     dx_ref, dw_ref, wbuf, bufy,
     dyv, pown, poth, wv, land,
-    ld_sem, dys_r, dyy_r, xs_r, w_r, ws_r, px_r, py_r, pf_r,
+    ld_sem, dys_r, dyy_r, xs_r, w_r, wp_r, ws_r, px_r, py_r, pf_r,
     s_dys, s_dyy, s_xs, s_w, s_ws, s_px, s_py, s_sum, wl_sem,
 ):
     row = lax.axis_index("row")
@@ -49,10 +49,10 @@
         return pl.ds(q * 256, 256)
 
     def xo(k0, n):
-        return dx_ref.at[:, pl.ds(pl.multiple_of(k0, 256), n)]
+        return dx_ref.at[:, pl.ds(pl.multiple_of(k0, 128), n)]
 
     def xs(k0, n):
-        return dx_ref.at[:, pl.ds(pl.multiple_of(2048 + k0, 256), n)]
+        return dx_ref.at[:, pl.ds(pl.multiple_of(2048 + k0, 128), n)]
 
     def dw_tile(q, kt, r0=0, n=512):
         return dw_ref.at[pl.ds(kt * 512 + r0, n), pl.ds(pl.multiple_of(q * 256, 256), 256)]
@@ -64,12 +64,15 @@
 
     def x_to_sib(kt):
         return remote(
-            x_ref.at[:, pl.ds((1 - c) * 2048 + kt * 512, 512)], xs(kt * 512, 512), s_xs.at[0], xs_r.at[1 + kt], sib
+            x_ref.at[:, pl.ds((1 - c) * 2048 + kt * 512, 512)], xs(kt * 512, 512), s_xs.at[0], xs_r.at[kt], sib
         )
 
-    def x_to_sib_half(h):
+    FIRST = ((0, 128), (128, 128), (256, 256))
+
+    def x_to_sib_part(i):
+        k0, n = FIRST[i]
         return remote(
-            x_ref.at[:, pl.ds((1 - c) * 2048 + h * 256, 256)], xs(h * 256, 256), s_xs.at[0], xs_r.at[h], sib
+            x_ref.at[:, pl.ds((1 - c) * 2048 + k0, n)], xs(k0, n), s_xs.at[0], xs_r.at[4 + i], sib
         )
 
     def dy_to_sib(j, q):
@@ -87,6 +90,15 @@
 
     def w_to_y(i):
         return remote(w_ref.at[rows(i)], wbuf.at[0, 1, rows(i)], s_w.at[0], w_r.at[1, i], yn)
+
+    def w_part(p):
+        return pl.ds(1024 + p * 64, 64)
+
+    def w_to_y_part(p):
+        return remote(w_ref.at[w_part(p)], wbuf.at[0, 1, w_part(p)], s_w.at[0], wp_r.at[p], yn)
+
+    def w_fwd_part(p):
+        return remote(wbuf.at[0, 1, w_part(p)], wbuf.at[0, 1, w_part(p)], s_w.at[0], wp_r.at[p], xn)
 
     def w_fwd(i):
         return remote(wbuf.at[0, 1, rows(i)], wbuf.at[0, 1, rows(i)], s_w.at[0], w_r.at[1, i], xn)
@@ -101,6 +113,12 @@
             px_r.at[q * 8 + kt * 2 + h], xn,
         )
 
+    def p_own_first(i):
+        k0, n = FIRST[i]
+        return remote(
+            pown.at[0, 0, pl.ds(k0, n)], dw_tile(0, 0, k0, n), s_px.at[0], px_r.at[(0, 32, 1)[i]], xn
+        )
+
     def p_own(q, kt):
         return remote(pown.at[q, kt], dw_tile(q, kt), s_px.at[0], px_r.at[16 + (q - 2) * 4 + kt], xn)
 
@@ -133,7 +151,7 @@
     pl.semaphore_wait(barrier, 3)
 
     dy_to_sib(0, 0).start()
-    x_to_sib_half(0).start()
+    x_to_sib_part(0).start()
     dy_to_y(0).start()
     dy_to_y(1).start()
 
@@ -146,11 +164,15 @@
 
     @pl.when(is_b)
     def _():
-        for i in range(8):
+        for i in range(4):
             w_to_y(i).start()
-        dy_to_y(2).start()
-
-    x_to_sib_half(1).start()
+        for q in range(2, 4):
+            dy_to_y(q).start()
+        for p in range(16):
+            w_to_y_part(p).start()
+
+    x_to_sib_part(1).start()
+    x_to_sib_part(2).start()
     for kt in range(1, 4):
         x_to_sib(kt).start()
     for q in range(1, 4):
@@ -162,29 +184,40 @@
             w_to_sib(0, i, True).start()
 
     def p_part(j, q, k0, n):
-        return _tdot(xo(k0, n)[...], dyv[0, j, :, q * 256:(q + 1) * 256]) + _tdot(
-            xs(k0, n)[...], dyv[1, j, :, q * 256:(q + 1) * 256]
-        )
+        def term(t, acc):
+            part = pl.ds(t * 1024, 1024)
+            cols = pl.ds(pl.multiple_of(k0, 128), n)
+            both = pl.ds(pl.multiple_of(2048 + k0, 128), n)
+            dy = pl.ds(q * 256, 256)
+            return acc + _tdot(dx_ref[part, cols], dyv[0, j, part, dy]) + _tdot(
+                dx_ref[part, both], dyv[1, j, part, dy]
+            )
+
+        return lax.fori_loop(0, 2, term, jnp.zeros((n, 256), F32), unroll=True)
 
     dy_load.wait()
     for q in range(4):
         dy_to_sib(0, q).wait_recv()
         if q == 0:
             x_load(0).wait()
-            for h in range(2):
-                x_to_sib_half(h).wait_recv()
-                pown[0, 0, h * 256:(h + 1) * 256] = p_part(0, 0, h * 256, 256)
+            for i, (k0, n) in enumerate(FIRST):
+                x_to_sib_part(i).wait_recv()
+                pown[0, 0, k0:k0 + n] = p_part(0, 0, k0, n)
 
                 @pl.when(is_b)
-                def _(h=h):
-                    p_own_half(0, 0, h).start()
+                def _(i=i):
+                    p_own_first(i).start()
 
         def own_body(kt, carry, q=q):
             if q == 0:
                 x_load(kt).wait()
                 x_to_sib(kt).wait_recv()
-            for h in range(2):
-                pown[q, kt, h * 256:(h + 1) * 256] = p_part(0, q, kt * 512 + h * 256, 256)
+
+            def half(h, carry):
+                pown[q, kt, pl.ds(h * 256, 256)] = p_part(0, q, kt * 512 + h * 256, 256)
+                return carry
+
+            lax.fori_loop(0, 2, half, 0)
             if q < 2:
                 @pl.when(is_b)
                 def _():
@@ -195,8 +228,11 @@
         lax.fori_loop(1 if q == 0 else 0, 4, own_body, 0)
 
     def other_tile(q, kt):
-        for h in range(2):
-            poth[q, kt, h * 256:(h + 1) * 256] = p_part(1, q, kt * 512 + h * 256, 256)
+        def half(h, carry):
+            poth[q, kt, pl.ds(h * 256, 256)] = p_part(1, q, kt * 512 + h * 256, 256)
+            return carry
+
+        lax.fori_loop(0, 2, half, 0)
 
     def trans_tile(q, kt):
         for r in range(4):
@@ -220,10 +256,6 @@
                 @pl.when(is_b)
                 def _():
                     trans_tile(q, kt)
-                    if q == 0:
-                        @pl.when(kt == 0)
-                        def _():
-                            dy_to_y(3).start()
             else:
                 @pl.when(is_b)
                 def _():
@@ -247,7 +279,7 @@
         for cp in w_loads(d, cc, own_from_arg):
             cp.wait()
 
-    def dx_stripe(d, cc):
+    def dx_stripe(d, cc, lo=0, hi=4):
         k0 = (c + cc * (1 - 2 * c)) * 2048
         cols = pl.ds(pl.multiple_of(k0 + d * 256, 256), 256)
 
@@ -258,7 +290,7 @@
             ).astype(BF16)
             return carry
 
-        lax.fori_loop(0, 4, body, 0)
+        lax.fori_loop(lo, hi, body, 0)
 
     def pair_wait(d, own_from_arg):
         w_to_sib(0, d, own_from_arg).wait_recv()
@@ -275,8 +307,16 @@
 
         def final_early(t):
             q, kt = t // 4, t % 4
-            for h in range(2):
-                p_own_half(q, kt, h).wait_recv()
+
+            @pl.when(t == 0)
+            def _():
+                for i in range(3):
+                    p_own_first(i).wait_recv()
+
+            @pl.when(t > 0)
+            def _():
+                for h in range(2):
+                    p_own_half(q, kt, h).wait_recv()
             add(q, kt)
 
         def final_late(t):
@@ -300,69 +340,79 @@
             final_early(i)
             return carry
 
-        lax.fori_loop(0, 8, early, 0)
+        lax.fori_loop(0, 4, early, 0)
 
         dy_in(2)
         dy_to_sib(1, 2).wait_recv()
 
         def q2_body(kt, carry):
             other_tile(2, kt)
-            a_sum(2, kt)
-            fwd(kt)
+            final_early(4 + kt)
             return carry
 
         lax.fori_loop(0, 4, q2_body, 0)
-
-        pair_wait(0, True)
         start_loads(0, 0, True)
         dy_in(3)
-        fwd(4)
-        dy_to_sib(1, 3).wait_recv()
-
-        def q3_body(kt, carry):
-            other_tile(3, kt)
-
-            @pl.when(kt < 3)
-            def _():
-                fwd(5 + kt)
-            return carry
-
-        lax.fori_loop(0, 4, q3_body, 0)
-
-        def late(d, carry):
-            @pl.when(d < 6)
-            def _():
-                fwd(4 * d + 8)
-            start_loads(d, 1, False)
-            wait_loads(d, 0, True)
-            dx_stripe(d, 0)
-
-            @pl.when(d < 6)
-            def _():
-                fwd(4 * d + 9)
-
-            @pl.when(d < 7)
-            def _():
-                pair_wait(d + 1, True)
-                start_loads(d + 1, 0, True)
-
-            @pl.when(d < 4)
-            def _():
-                a_sum(3, d)
-
-            @pl.when(d < 6)
-            def _():
-                fwd(4 * d + 10)
-            wait_loads(d, 1, False)
-            dx_stripe(d, 1)
-
-            @pl.when(d < 6)
-            def _():
-                fwd(4 * d + 11)
-                final_late(d)
-            return carry
-
-        lax.fori_loop(0, 8, late, 0)
+
+        def step(i, carry):
+            @pl.when(i < 16)
+            def _():
+                w_to_y_part(i).wait_recv()
+                w_fwd_part(i).start()
+
+                @pl.when(i % 4 == 3)
+                def _():
+                    w_to_sib(1, 4 + i // 4, False).start()
+
+            @pl.when(i >= 16)
+            def _():
+                fwd(i - 16)
+
+            @pl.when(i == 0)
+            def _():
+                dy_to_sib(1, 3).wait_recv()
+
+            @pl.when(i < 4)
+            def _():
+                other_tile(3, i)
+
+            @pl.when(jnp.logical_and(i >= 4, i < 36))
+            def _():
+                e = (i - 4) // 2
+                d, cc = e // 2, e % 2
+                odd = i % 2
+
+                @pl.when(odd == 0)
+                def _():
+                    @pl.when(cc == 0)
+                    def _():
+                        pair_wait(d, True)
+                        start_loads(d, 1, False)
+                        wait_loads(d, 0, True)
+
+                    @pl.when(cc == 1)
+                    def _():
+                        @pl.when(d < 7)
+                        def _():
+                            start_loads(d + 1, 0, True)
+                        wait_loads(d, 1, False)
+
+                dx_stripe(d, cc, 2 * odd, 2 * odd + 2)
+
+            @pl.when(jnp.logical_and(i < 8, i % 2 == 1))
+            def _():
+                a_sum(2, i // 2)
+
+            @pl.when(jnp.logical_and(jnp.logical_and(i >= 10, i < 26), i % 4 == 2))
+            def _():
+                a_sum(3, (i - 10) // 4)
+
+            @pl.when(jnp.logical_and(i >= 26, i % 4 == 2))
+            def _():
+                final_late((i - 26) // 4)
+            return carry
+
+        lax.fori_loop(0, 48, step, 0)
         final_late(6)
         final_late(7)
         remote(wbuf.at[0], wbuf.at[0], s_w.at[0], w_r.at[0, 0], xn).wait_send()
@@ -386,7 +436,14 @@
         lax.fori_loop(0, 8, own_w, 0)
 
         def stripes(d, carry):
-            w_to_y(d).wait_recv()
+            @pl.when(d < 4)
+            def _():
+                w_to_y(d).wait_recv()
+
+            @pl.when(d >= 4)
+            def _():
+                for p in range(4):
+                    w_to_y_part(4 * (d - 4) + p).wait_recv()
             w_to_sib(1, d, False).start()
             start_loads(d, 0, False)
             pair_wait(d, False)
@@ -457,7 +514,8 @@
             pltpu.VMEM((4, 4, 512, 256), F32),
             pltpu.VMEM((2, 2, 256, 1024), BF16),
             pltpu.VMEM((2, 4, 512, 256), F32),
-            dma((5,)), dma((2, 4)), dma((4,)), dma((5,)), dma((2, 8)), dma((2, 8)), dma((32,)), dma((16,)), dma((32,)),
+            dma((5,)), dma((2, 4)), dma((4,)), dma((7,)), dma((2, 8)), dma((16,)), dma((2, 8)), dma((33,)), dma((16,)),
+            dma((32,)),
             dma((1,)), dma((1,)), dma((1,)), dma((1,)), dma((1,)), dma((2,)), dma((1,)), dma((1,)), dma((2, 2)),
         ],
         compiler_params=pltpu.CompilerParams(

time: 300 us -> 290 us (0.967)
  Pallas kernels: 299 us -> 289 us
    pallas_call x1, Pallas kernels: 290 us -> 281 us  [local_backward(): pl.pallas_call(kernel, out_shape=(pltpu.VMEM((2048, 4096), BF16), pltpu.V...]
where the time goes in v4:
time: 290 us
  Pallas kernels  289 us (100%)
    pallas_call x1, Pallas kernels, local_backward(): pl.pallas_call(kernel, out_shape=(pltpu.VMEM((2048, 4096), BF16), pltpu.V...  281 us
    pallas_call x1, Pallas kernels, local_backward(): pl.pallas_call(store_kernel, out_shape=(jax.ShapeDtypeStruct((2048, 4096)...  8.45 us

profile of v4, /device:TPU:0, one launch (start us, length us, event | category | flops | bytes accessed | tf_op | source)
XLA Modules:
  0.0 290.2 jit_solution(4579260235657034288)
XLA Ops:
  0.6 281.0 %shard_map.50 = (bf16[2048,4096]{1,0:T(8,128)(2,1)S(1)}, f32[2048,1024]{1,0:T(8,128)S(1)}, bf16[2,2,2048,1024]{3,2,1,0:T(8,128)(2,1)}, f32[2,4,512,256]{3,2,1,0:T(8,128)}) custom-call(bf16[2048,4096]{1,0:T(8,128)(2,1)} %x_ref.1, bf16[2048,1024]{1,0:T(8,128)(2,1)} %w_ref.1, bf16[2048,1024]{1,0:T(8,128)(2,1)} %dy_ref.1), custom_call_target="tpu_custom_call" | custom-call | flops 68719476736 | bytes 104857600 | tf_op jit(solution)/shard_map/pallas_call | solution.py:501
  281.6 8.4 %shard_map.51 = (bf16[2048,4096]{1,0:T(8,128)(2,1)}, f32[2048,1024]{1,0:T(8,128)}) custom-call(bf16[2048,4096]{1,0:T(8,128)(2,1)S(1)} %get-tuple-element.4.dx_ref, f32[2048,1024]{1,0:T(8,128)S(1)} %get-tuple-element.5.dw_ref), custom_call_target="tpu_custom_call" | custom-call | bytes 50331648 | tf_op jit(solution)/shard_map/pallas_call | solution.py:526

commit v5 on v4

--- a/solution.py
+++ b/solution.py
@@ -22,10 +22,10 @@
 
 def kernel(
     x_ref, w_ref, dy_ref,
-    dx_ref, dw_ref, wbuf, bufy,
+    dx_ref, dw_ref, wbuf, bufy, tail,
     dyv, pown, poth, wv, land,
     ld_sem, dys_r, dyy_r, xs_r, w_r, wp_r, ws_r, px_r, py_r, pf_r,
-    s_dys, s_dyy, s_xs, s_w, s_ws, s_px, s_py, s_sum, wl_sem,
+    s_dys, s_dyy, s_xs, s_w, s_ws, s_px, s_py, s_sum, wl_sem, tail_sem,
 ):
     row = lax.axis_index("row")
     y = lax.axis_index("col")
@@ -122,6 +122,14 @@
     def p_own(q, kt):
         return remote(pown.at[q, kt], dw_tile(q, kt), s_px.at[0], px_r.at[16 + (q - 2) * 4 + kt], xn)
 
+    def p_own_last():
+        return remote(
+            pown.at[3, 3, pl.ds(0, 256)], dw_tile(3, 3, 0, 256), s_px.at[0], px_r.at[23], xn
+        )
+
+    def tail_store():
+        return local(pown.at[3, 3, pl.ds(256, 256)], tail, tail_sem.at[0])
+
     def p_other(q, kt):
         return remote(poth.at[q, kt], land.at[q - 2, kt], s_px.at[1], px_r.at[24 + (q - 2) * 4 + kt], xn)
 
@@ -129,6 +137,12 @@
         q, kt, r = i // 16, (i // 4) % 4, i % 4
         part = pl.ds(r * 128, 128)
         return remote(poth.at[q, kt, part], bufy.at[q, kt, part], s_py.at[0], pf_r.at[i], yn)
+
+    def p_trans_tail(i):
+        return remote(
+            poth.at[1, 3, pl.ds(i * 128 - 3584, 128)], tail.at[pl.ds((i - 30) * 128, 128)],
+            s_py.at[0], pf_r.at[i], yn,
+        )
 
     def p_fwd(i):
         q, kt, r = i // 16, (i // 4) % 4, i % 4
@@ -236,7 +250,16 @@
 
     def trans_tile(q, kt):
         for r in range(4):
-            p_trans(16 * q + 4 * kt + r).start()
+            if q == 1 and r >= 2:
+                @pl.when(kt < 3)
+                def _(r=r):
+                    p_trans(16 * q + 4 * kt + r).start()
+
+                @pl.when(kt == 3)
+                def _(r=r):
+                    p_trans_tail(28 + r).start()
+            else:
+                p_trans(16 * q + 4 * kt + r).start()
 
     def dy_in(q):
         dy_to_y(q).wait_recv()
@@ -412,11 +435,19 @@
                 final_late((i - 26) // 4)
             return carry
 
-        lax.fori_loop(0, 48, step, 0)
+        lax.fori_loop(0, 46, step, 0)
+        final_late(5)
         final_late(6)
-        final_late(7)
+        low = dw_tile(3, 3, 256, 256)
+        low[...] = pown[3, 3, 256:512]
+        for i in (30, 31):
+            p_trans_tail(i).wait_recv()
+        p_own_last().wait_recv()
+        top = dw_tile(3, 3, 0, 256)
+        top[...] = top[...] + pown[3, 3, 0:256]
         remote(wbuf.at[0], wbuf.at[0], s_w.at[0], w_r.at[0, 0], xn).wait_send()
-        remote(land, land, s_px.at[0], px_r.at[0], xn).wait_send()
+        sent = dyv.at[0, 0, pl.ds(0, 1920)]
+        remote(sent, sent, s_px.at[0], px_r.at[0], xn).wait_send()
         remote(land, land, s_py.at[0], py_r.at[0], yn).wait_send()
         remote(land, land, s_sum.at[0], py_r.at[0], yn).wait_send()
 
@@ -426,7 +457,11 @@
         other_pass(3)
         for q in range(2, 4):
             for kt in range(4):
-                p_own(q, kt).start()
+                if q == 3 and kt == 3:
+                    p_own_last().start()
+                    tail_store().start()
+                else:
+                    p_own(q, kt).start()
 
         def own_w(i, carry):
             w_own_to_x(i).wait_recv()
@@ -467,12 +502,14 @@
             tile[...] = tile[...] + land[q, kt, pl.ds(r * 128, 128)]
             return carry
 
-        lax.fori_loop(0, 32, fin, 0)
+        lax.fori_loop(0, 30, fin, 0)
         for q in range(2, 4):
             for kt in range(4):
                 sum_to_y(q, kt).wait_recv()
         remote(wbuf.at[0, 0], wbuf.at[0, 0], s_w.at[0], w_r.at[0, 0], yn).wait_send()
-        remote(pown, pown, s_px.at[0], px_r.at[0], xn).wait_send()
+        tail_store().wait()
+        sent = dw_ref.at[pl.ds(0, 1984)]
+        remote(sent, sent, s_px.at[0], px_r.at[0], xn).wait_send()
         remote(land, land, s_px.at[1], px_r.at[0], xn).wait_send()
         remote(land, land, s_py.at[0], py_r.at[0], yn).wait_send()
 
@@ -492,6 +529,16 @@
         cp.start()
     for cp in copies:
         cp.wait()
+
+
+def add_kernel(done_ref, dw_ref, tail_ref, dw_out, buf, sem):
+    is_a = lax.axis_index("row") // 2 == lax.axis_index("col")
+    col = jnp.where(is_a, 768, 256)
+    cols = pl.ds(pl.multiple_of(col, 256), 256)
+    buf[...] = dw_ref[1792:2048, cols] + tail_ref[...]
+    cp = pltpu.make_async_copy(buf, dw_out.at[pl.ds(1792, 256), cols], sem.at[0])
+    cp.start()
+    cp.wait()
 
 
 def local_backward(act_blk, w_blk, grad_blk):
@@ -505,9 +552,10 @@
             pltpu.VMEM((2048, 1024), F32),
             jax.ShapeDtypeStruct((2, 2, 2048, 1024), BF16),
             jax.ShapeDtypeStruct((2, 4, 512, 256), F32),
+            jax.ShapeDtypeStruct((256, 256), F32),
         ),
         in_specs=[any_spec] * 3,
-        out_specs=(vmem_spec, vmem_spec) + (any_spec,) * 2,
+        out_specs=(vmem_spec, vmem_spec) + (any_spec,) * 3,
         scratch_shapes=[
             pltpu.VMEM((2, 2, 2048, 1024), BF16),
             pltpu.VMEM((4, 4, 512, 256), F32),
@@ -516,14 +564,15 @@
             pltpu.VMEM((2, 4, 512, 256), F32),
             dma((5,)), dma((2, 4)), dma((4,)), dma((7,)), dma((2, 8)), dma((16,)), dma((2, 8)), dma((33,)), dma((16,)),
             dma((32,)),
-            dma((1,)), dma((1,)), dma((1,)), dma((1,)), dma((1,)), dma((2,)), dma((1,)), dma((1,)), dma((2, 2)),
+            dma((1,)), dma((1,)), dma((1,)), dma((1,)), dma((1,)), dma((2,)), dma((1,)), dma((1,)), dma((2, 2)), dma((1,)),
         ],
         compiler_params=pltpu.CompilerParams(
             collective_id=0, has_side_effects=True, vmem_limit_bytes=41_800_000
         ),
         cost_estimate=pl.CostEstimate(flops=2 * 2048 * 2048 * 4096 * 2, bytes_accessed=100 << 20, transcendentals=0),
     )(act_blk, w_blk, grad_blk)
-    return pl.pallas_call(
+    tail = lax.ppermute(outs[4], "row", [(0, 2), (1, 3), (2, 0), (3, 1)])
+    dx, dw = pl.pallas_call(
         store_kernel,
         out_shape=(jax.ShapeDtypeStruct((2048, 4096), BF16), jax.ShapeDtypeStruct((2048, 1024), F32)),
         in_specs=[vmem_spec, vmem_spec],
@@ -532,6 +581,17 @@
         compiler_params=pltpu.CompilerParams(vmem_limit_bytes=1 << 20),
         cost_estimate=pl.CostEstimate(flops=0, bytes_accessed=48 << 20, transcendentals=0),
     )(outs[0], outs[1])
+    dw = pl.pallas_call(
+        add_kernel,
+        out_shape=jax.ShapeDtypeStruct((2048, 1024), F32),
+        in_specs=[any_spec, vmem_spec, vmem_spec],
+        out_specs=any_spec,
+        scratch_shapes=[pltpu.VMEM((256, 256), F32), dma((1,))],
+        input_output_aliases={0: 0},
+        compiler_params=pltpu.CompilerParams(vmem_limit_bytes=2 << 20),
+        cost_estimate=pl.CostEstimate(flops=0, bytes_accessed=1 << 20, transcendentals=0),
+    )(dw, outs[1], tail)
+    return dx, dw
 
 
 def solution(mesh):

time: 290 us -> 288 us (level)
  Pallas kernels: 289 us -> 286 us
    pallas_call x1, Pallas kernels: 281 us -> 277 us  [local_backward(): pl.pallas_call(kernel, out_shape=(pltpu.VMEM((2048, 4096), BF16), pltpu.V...]
  transfers between devices with their start and end apart: 0 -> 1, of which waited for: 0 -> 0; matrix products, arithmetic and copies ran while one was open for 0% -> 0% of each run, Pallas kernels for 0% -> 3%
where the time goes in v5:
time: 288 us
  Pallas kernels  286 us (99%)
    pallas_call x1, Pallas kernels, local_backward(): pl.pallas_call(kernel, out_shape=(pltpu.VMEM((2048, 4096), BF16), pltpu.V...  277 us
    pallas_call x1, Pallas kernels, local_backward(): pl.pallas_call(store_kernel, out_shape=(jax.ShapeDtypeStruct((2048, 4096)...  8.44 us
  transfers between devices with their start and end apart: 1, of which 0 were waited for; matrix products, arithmetic and copies ran while one was open for 0% of the time, Pallas kernels for 3%

profile of v5, /device:TPU:0, one launch (start us, length us, event | category | flops | bytes accessed | tf_op | source)
XLA Modules:
  0.0 287.6 jit_solution(490746443007057756)
XLA Ops:
  0.6 277.0 %shard_map.50 = (bf16[2048,4096]{1,0:T(8,128)(2,1)S(1)}, f32[2048,1024]{1,0:T(8,128)S(1)}, bf16[2,2,2048,1024]{3,2,1,0:T(8,128)(2,1)}, f32[2,4,512,256]{3,2,1,0:T(8,128)}, f32[256,256]{1,0:T(8,128)}) custom-call(bf16[2048,4096]{1,0:T(8,128)(2,1)} %x_ref.1, bf16[2048,1024]{1,0:T(8,128)(2,1)} %w_ref.1, bf16[2048,1024]{1,0:T(8,128)(2,1)} %dy_ref.1), custom_call_target="tpu_custom_call" | custom-call | flops 68719476736 | bytes 104857600 | tf_op jit(solution)/shard_map/pallas_call | solution.py:548
  277.6 0.6 collective-permute-start
  278.2 8.4 %shard_map.51 = (bf16[2048,4096]{1,0:T(8,128)(2,1)}, f32[2048,1024]{1,0:T(8,128)}) custom-call(bf16[2048,4096]{1,0:T(8,128)(2,1)S(1)} %get-tuple-element.7.dx_ref, f32[2048,1024]{1,0:T(8,128)S(1)} %get-tuple-element.8.dw_ref), custom_call_target="tpu_custom_call" | custom-call | bytes 50331648 | tf_op jit(solution)/shard_map/pallas_call | solution.py:575
  286.7 0.0 collective-permute-done.tail_ref
  286.7 0.8 shard_map.52
Async XLA Ops:
  277.6 9.1 %collective-permute-start = (f32[256,256]{1,0:T(8,128)}, f32[256,256]{1,0:T(8,128)S(1)}, u32[]{:S(2)}, u32[]{:S(2)}) collective-permute-start(f32[256,256]{1,0:T(8,128)} %get-tuple-element.11), channel_id=1, source_target_pairs={{0,2},{1,3},{2,0},{3,1},{4,6},{5,7},{6,4},{7,5}} | collective-permute-start | bytes 786440 | tf_op jit(solution)/shard_map/ppermute | solution.py:574

commit v6 on v0

v6 whole, which is shorter than its diff:
```python
import jax
import jax.numpy as jnp
from jax import lax
from jax.experimental import pallas as pl
from jax.experimental.pallas import tpu as pltpu
from jax.sharding import PartitionSpec as P

MESH = pl.DeviceIdType.MESH
F32 = jnp.float32
BF16 = jnp.bfloat16
H, N, D, T, Q, S = 2048, 1024, 512, 256, 128, 64
R = 320
ME, SIB = 0, 1
OWN, OTH = 0, 1
ARG, BUF = "arg", "buf"
FIRST = ((0, Q, 0, Q), (0, Q, Q, Q), (Q, Q, 0, T), (T, T, 0, T))


def _tdot(a, b):
    return lax.dot_general(a, b, (((0,), (0,)), ((), ())), preferred_element_type=F32)


def _dot_t(a, b):
    return lax.dot_general(a, b, (((1,), (1,)), ((), ())), preferred_element_type=F32)


def loop(n, f, start=0):
    def body(i, carry):
        f(i)
        return carry

    lax.fori_loop(start, n, body, start)


def cut(k0, n, unit=Q):
    return pl.ds(pl.multiple_of(k0, unit), n)


def kernel(
    x_ref, w_ref, dy_ref,
    dx_ref, dw_ref, wbuf, bufy, tail,
    dyv, pown, poth, wv, land,
    dy_sem, x_sem, dys_r, dyy_r, xs_r, xf_r, w_r, wp_r, ws_r, pa_r, ph_r, po_r, ps_r, py_r, pf_r,
    s_dys, s_dyy, s_xs, s_w, s_ws, s_px, s_po, s_py, s_sum, wl_sem, tail_sem,
):
    row = lax.axis_index("row")
    y = lax.axis_index("col")
    x = row // 2
    c = row % 2
    is_a = x == y
    is_b = x != y
    sib = {"row": row + 1 - 2 * c}
    xn = {"row": (row + 2) % 4}
    yn = {"col": 1 - y}

    def remote(src, dst, ssem, rsem, dev):
        return pltpu.make_async_remote_copy(
            src_ref=src, dst_ref=dst, send_sem=ssem, recv_sem=rsem, device_id=dev, device_id_type=MESH
        )

    def local(src, dst, sem):
        return pltpu.make_async_copy(src, dst, sem)

    def qs(q):
        return pl.ds(q * T, T)

    def xo(k0, n):
        return dx_ref.at[:, cut(k0, n)]

    def xs(k0, n):
        return dx_ref.at[:, cut(H + k0, n)]

    def dw_part(q, r0, n):
        return dw_ref.at[pl.ds(r0, n), cut(q * T, T)]

    def dw_tile(q, kt):
        return dw_part(q, kt * D, D)

    dy_load = local(dy_ref, dyv.at[ME, OWN], dy_sem)

    def x_load(kt):
        return local(x_ref.at[:, pl.ds(c * H + kt * D, D)], xo(kt * D, D), x_sem.at[kt])

    def x_cols_to_sib(k0, n, sem):
        return remote(x_ref.at[:, pl.ds((1 - c) * H + k0, n)], xs(k0, n), s_xs, sem, sib)

    def x_to_sib(kt):
        return x_cols_to_sib(kt * D, D, xs_r.at[kt])

    def x_first(i):
        k0, n = ((0, Q), (Q, Q), (T, T))[i]
        return x_cols_to_sib(k0, n, xf_r.at[i])

    def dy_first(i):
        cols = pl.ds(i * Q, Q)
        return remote(dy_ref.at[:, cols], dyv.at[SIB, OWN, :, cols], s_dys, xf_r.at[3 + i], sib)

    def dy_to_sib(j, q):
        src = dy_ref.at[:, qs(q)] if j == OWN else dyv.at[ME, OTH, :, qs(q)]
        return remote(src, dyv.at[SIB, j, :, qs(q)], s_dys, dys_r.at[j, q], sib)

    def dy_to_y(q):
        return remote(dy_ref.at[:, qs(q)], dyv.at[ME, OTH, :, qs(q)], s_dyy, dyy_r.at[q], yn)

    def w_own_to_x(i):
        return remote(w_ref.at[qs(i)], wbuf.at[ME, OWN, qs(i)], s_w, w_r.at[OWN, i], xn)

    def w_to_y(i):
        return remote(w_ref.at[qs(i)], wbuf.at[ME, OTH, qs(i)], s_w, w_r.at[OTH, i], yn)

    def w_fwd(i):
        return remote(wbuf.at[ME, OTH, qs(i)], wbuf.at[ME, OTH, qs(i)], s_w, w_r.at[OTH, i], xn)

    def w_piece(p):
        return pl.ds(N + p * S, S)

    def w_to_y_piece(p):
        return remote(w_ref.at[w_piece(p)], wbuf.at[ME, OTH, w_piece(p)], s_w, wp_r.at[p], yn)

    def w_fwd_piece(p):
        return remote(wbuf.at[ME, OTH, w_piece(p)], wbuf.at[ME, OTH, w_piece(p)], s_w, wp_r.at[p], xn)

    def w_to_sib(j, i, src):
        ref = w_ref.at[qs(i)] if src == ARG else wbuf.at[ME, j, qs(i)]
        return remote(ref, wbuf.at[SIB, j, qs(i)], s_ws, ws_r.at[j, i], sib)

    def p_first(i):
        r0, n, c0, m = FIRST[i]
        return remote(
            pown.at[0, 0, pl.ds(r0, n), pl.ds(c0, m)], dw_ref.at[pl.ds(r0, n), pl.ds(c0, m)],
            s_px, pa_r.at[i], xn,
        )

    def p_half(q, kt, h):
        return remote(
            pown.at[q, kt, pl.ds(h * T, T)], dw_part(q, kt * D + h * T, T), s_px, ph_r.at[q, 2 * kt + h], xn
        )

    def p_own(q, kt):
        return remote(pown.at[q, kt], dw_tile(q, kt), s_px, po_r.at[q - 2, kt], xn)

    def p_own_last():
        return remote(
            pown.at[3, 3, pl.ds(0, D - R)], dw_part(3, 3 * D, D - R), s_px, po_r.at[1, 3], xn
        )

    def tail_store():
        return local(pown.at[3, 3, pl.ds(D - R, R)], tail, tail_sem)

    def p_other(q, kt):
        return remote(poth.at[q, kt], land.at[q - 2, kt], s_po, ps_r.at[q - 2, kt], xn)

    def p_trans(q, kt, r):
        part = pl.ds(r * Q, Q)
        return remote(poth.at[q, kt, part], bufy.at[q, kt, part], s_py, pf_r.at[q, 4 * kt + r], yn)

    def p_fwd(q, kt, r):
        part = pl.ds(r * Q, Q)
        return remote(bufy.at[q, kt, part], land.at[q, kt, part], s_px, pf_r.at[q, 4 * kt + r], xn)

    def p_trans_short():
        part = pl.ds(Q, S)
        return remote(poth.at[1, 3, part], bufy.at[1, 3, part], s_py, pf_r.at[1, 13], yn)

    def p_fwd_short():
        part = pl.ds(Q, S)
        return remote(bufy.at[1, 3, part], land.at[1, 3, part], s_px, pf_r.at[1, 13], xn)

    def p_trans_tail():
        return remote(poth.at[1, 3, pl.ds(D - R, R)], tail, s_py, pf_r.at[1, 14], yn)

    def p_term(q, kt):
        return remote(poth.at[q, kt], dw_tile(q, kt), s_py, py_r.at[q, kt], yn)

    def sum_to_y(q, kt):
        return remote(poth.at[q, kt], dw_tile(q, kt), s_sum, py_r.at[q, kt], yn)

    def drain(ref, sem):
        remote(ref, ref, sem, dyy_r.at[0], yn).wait_send()

    dy_load.start()
    for kt in range(4):
        x_load(kt).start()

    barrier = pltpu.get_barrier_semaphore()
    for dev in (sib, xn, yn):
        pl.semaphore_signal(barrier, inc=1, device_id=dev, device_id_type=MESH)
    pl.semaphore_wait(barrier, 3)

    dy_first(0).start()
    x_first(0).start()
    dy_to_y(0).start()
    dy_first(1).start()
    x_first(1).start()
    x_first(2).start()
    dy_to_y(1).start()

    @pl.when(is_a)
    def _():
        for i in range(8):
            w_own_to_x(i).start()
        for q in (2, 3):
            dy_to_y(q).start()

    @pl.when(is_b)
    def _():
        for i in range(4):
            w_to_y(i).start()
        for q in (2, 3):
            dy_to_y(q).start()
        for p in range(16):
            w_to_y_piece(p).start()

    for kt in (1, 2, 3):
        x_to_sib(kt).start()
    for q in (1, 2, 3):
        dy_to_sib(OWN, q).start()

    @pl.when(is_a)
    def _():
        for i in range(8):
            w_to_sib(OWN, i, ARG).start()

    def p_part(j, c0, k0, n, m=T):
        dy = pl.ds(c0, m)
        acc = None
        for t in range(2):
            part = pl.ds(t * N, N)
            for who, base in ((ME, k0), (SIB, H + k0)):
                term = _tdot(dx_ref[part, cut(base, n)], dyv[who, j, part, dy])
                acc = term if acc is None else acc + term
        return acc

    def p_tile(dst, j, q, kt):
        loop(2, lambda h: put(dst.at[q, kt, pl.ds(h * T, T)], p_part(j, q * T, kt * D + h * T, T)))

    def put(ref, value):
        ref[...] = value

    dy_load.wait()
    x_load(0).wait()
    dy_first(0).wait_recv()
    for i, (r0, n, c0, m) in enumerate(FIRST):
        if i == 1:
            dy_first(1).wait_recv()
        else:
            x_first(max(i - 1, 0)).wait_recv()
        put(pown.at[0, 0, pl.ds(r0, n), pl.ds(c0, m)], p_part(OWN, c0, r0, n, m))

        @pl.when(is_b)
        def _(i=i):
            p_first(i).start()

    def own_tile(q, kt):
        if q == 0:
            x_load(kt).wait()
            x_to_sib(kt).wait_recv()
        p_tile(pown, OWN, q, kt)
        if q < 2:
            @pl.when(is_b)
            def _():
                p_half(q, kt, 0).start()
                p_half(q, kt, 1).start()

    for q in range(4):
        if q > 0:
            dy_to_sib(OWN, q).wait_recv()
        loop(4, lambda kt, q=q: own_tile(q, kt), int(q == 0))

    def trans_tile(q, kt):
        if q == 0:
            for r in range(4):
                p_trans(q, kt, r).start()
            return
        p_trans(q, kt, 0).start()

        @pl.when(kt < 3)
        def _():
            for r in (1, 2, 3):
                p_trans(q, kt, r).start()

        @pl.when(kt == 3)
        def _():
            p_trans_short().start()
            p_trans_tail().start()

    def dy_in(q):
        dy_to_y(q).wait_recv()
        dy_to_sib(OTH, q).start()

    def other_pass(q):
        dy_in(q)
        dy_to_sib(OTH, q).wait_recv()

        def tile(kt):
            p_tile(poth, OTH, q, kt)
            if q < 2:
                @pl.when(is_a)
                def _():
                    p_term(q, kt).start()

                @pl.when(is_b)
                def _():
                    trans_tile(q, kt)
            else:
                @pl.when(is_b)
                def _():
                    p_other(q, kt).start()

        loop(4, tile)

    def w_loads(d, cc, src):
        ref = w_ref.at[qs(d)] if src == ARG else wbuf.at[cc, OWN, qs(d)]
        return (
            local(ref, wv.at[cc, OWN], wl_sem.at[cc, OWN]),
            local(wbuf.at[cc, OTH, qs(d)], wv.at[cc, OTH], wl_sem.at[cc, OTH]),
        )

    def start_loads(d, cc, src):
        for cp in w_loads(d, cc, src):
            cp.start()

    def wait_loads(d, cc, src):
        for cp in w_loads(d, cc, src):
            cp.wait()

    def dx_stripe(d, cc, lo=0, hi=4):
        cols = cut((c + cc * (1 - 2 * c)) * H + d * T, T, T)

        def rows(m):
            part = pl.ds(m * D, D)
            dx_ref[part, cols] = (
                _dot_t(dyv[ME, OWN, part, :], wv[cc, OWN]) + _dot_t(dyv[ME, OTH, part, :], wv[cc, OTH])
            ).astype(BF16)

        loop(hi, rows, lo)

    def pair_wait(d, src):
        w_to_sib(OWN, d, src).wait_recv()
        w_to_sib(OTH, d, BUF).wait_recv()

    other_pass(0)
    other_pass(1)

    @pl.when(is_a)
    def _():
        def add(q, kt):
            tile = dw_tile(q, kt)
            tile[...] = tile[...] + pown[q, kt]

        def final_early(t):
            q, kt = t // 4, t % 4

            @pl.when(t == 0)
            def _():
                for i in range(len(FIRST)):
                    p_first(i).wait_recv()

            @pl.when(t > 0)
            def _():
                p_half(q, kt, 0).wait_recv()
                p_half(q, kt, 1).wait_recv()
            add(q, kt)

        def final_late(t):
            q, kt = 2 + t // 4, t % 4
            p_own(q, kt).wait_recv()
            add(q, kt)

        def a_sum(q, kt):
            p_other(q, kt).wait_recv()
            poth[q, kt] = poth[q, kt] + land[q - 2, kt]
            sum_to_y(q, kt).start()

        def early(i):
            w_to_y(i).wait_recv()
            w_fwd(i).start()
            w_to_sib(OTH, i, BUF).start()
            final_early(i)

        loop(4, early)
        dy_in(2)
        dy_to_sib(OTH, 2).wait_recv()

        def q2_tile(kt):
            p_tile(poth, OTH, 2, kt)
            final_early(4 + kt)

        loop(4, q2_tile)
        start_loads(0, ME, ARG)
        dy_in(3)

        def step(i):
            @pl.when(i < 16)
            def _():
                w_to_y_piece(i).wait_recv()
                w_fwd_piece(i).start()

                @pl.when(i % 4 == 3)
                def _():
                    w_to_sib(OTH, 4 + i // 4, BUF).start()

            @pl.when(i >= 16)
            def _():
                k = i - 16
                q, kt, r = k // 16, (k // 4) % 4, k % 4
                p_trans(q, kt, r).wait_recv()
                p_fwd(q, kt, r).start()

            @pl.when(i == 0)
            def _():
                dy_to_sib(OTH, 3).wait_recv()

            @pl.when(i < 4)
            def _():
                p_tile(poth, OTH, 3, i)

            @pl.when(jnp.logical_and(i >= 4, i < 36))
            def _():
                e = (i - 4) // 2
                d, cc = e // 2, e % 2
                odd = i % 2

                @pl.when(jnp.logical_and(odd == 0, cc == ME))
                def _():
                    pair_wait(d, ARG)
                    start_loads(d, SIB, BUF)
                    wait_loads(d, ME, ARG)

                @pl.when(jnp.logical_and(odd == 0, cc == SIB))
                def _():
                    @pl.when(d < 7)
                    def _():
                        start_loads(d + 1, ME, ARG)
                    wait_loads(d, SIB, BUF)

                dx_stripe(d, cc, 2 * odd, 2 * odd + 2)

            @pl.when(jnp.logical_and(i < 8, i % 2 == 1))
            def _():
                a_sum(2, i // 2)

            @pl.when(jnp.logical_and(jnp.logical_and(i >= 10, i < 26), i % 4 == 2))
            def _():
                a_sum(3, (i - 10) // 4)

            @pl.when(jnp.logical_and(i >= 26, i % 4 == 2))
            def _():
                final_late((i - 26) // 4)

        loop(45, step)
        p_trans_short().wait_recv()
        p_fwd_short().start()
        low = dw_part(3, 4 * D - R, R)
        low[...] = pown[3, 3, D - R:]
        final_late(5)
        final_late(6)
        p_trans_tail().wait_recv()
        p_own_last().wait_recv()
        top = dw_part(3, 3 * D, D - R)
        top[...] = top[...] + pown[3, 3, :D - R]
        drain(wbuf.at[ME], s_w)
        drain(dyv.at[ME, OWN, pl.ds(0, H - R // 2)], s_px)
        drain(land, s_py)
        drain(land, s_sum)

    @pl.when(is_b)
    def _():
        other_pass(2)
        other_pass(3)
        for t in range(7):
            p_own(2 + t // 4, t % 4).start()
        p_own_last().start()
        tail_store().start()

        def own_w(i):
            w_own_to_x(i).wait_recv()
            w_to_sib(OWN, i, BUF).start()

        loop(8, own_w)

        def stripes(d):
            @pl.when(d < 4)
            def _():
                w_to_y(d).wait_recv()

            @pl.when(d >= 4)
            def _():
                for p in range(4):
                    w_to_y_piece(4 * (d - 4) + p).wait_recv()
            w_to_sib(OTH, d, BUF).start()
            start_loads(d, ME, BUF)
            pair_wait(d, BUF)
            start_loads(d, SIB, BUF)
            for cc in (ME, SIB):
                wait_loads(d, cc, BUF)
                dx_stripe(d, cc)

        loop(8, stripes)

        def fin(i):
            q, kt, r = i // 16, (i // 4) % 4, i % 4

            @pl.when(r == 0)
            def _():
                p_term(q, kt).wait_recv()
            p_fwd(q, kt, r).wait_recv()
            tile = dw_part(q, kt * D + r * Q, Q)
            tile[...] = tile[...] + land[q, kt, pl.ds(r * Q, Q)]

        loop(29, fin)
        p_fwd_short().wait_recv()
        tile = dw_part(1, 3 * D + Q, S)
        tile[...] = tile[...] + land[1, 3, Q:Q + S]
        for q in (2, 3):
            for kt in range(4):
                sum_to_y(q, kt).wait_recv()
        tail_store().wait()
        drain(wbuf.at[ME, OWN], s_w)
        drain(dw_ref.at[pl.ds(0, H - R // 4)], s_px)
        drain(land, s_po)
        drain(land, s_py)

    drain(dyv.at[ME], s_dys)
    drain(dyv.at[ME, OWN], s_dyy)
    drain(wbuf.at[ME], s_xs)
    drain(wbuf.at[ME], s_ws)


def store_kernel(dx_ref, dw_ref, dx_out, dw_out, sem):
    copies = []
    for i in range(4):
        part = pl.ds(i * D, D)
        copies.append(pltpu.make_async_copy(dx_ref.at[part], dx_out.at[part], sem.at[0, i]))
        copies.append(pltpu.make_async_copy(dw_ref.at[part], dw_out.at[part], sem.at[1, i]))
    for cp in copies:
        cp.start()
    for cp in copies:
        cp.wait()


def add_kernel(done_ref, dw_ref, tail_ref, dw_out, buf, sem):
    is_a = lax.axis_index("row") // 2 == lax.axis_index("col")
    cols = cut(jnp.where(is_a, 3 * T, T), T)
    buf[...] = dw_ref[H - R:, cols] + tail_ref[...]
    cp = pltpu.make_async_copy(buf, dw_out.at[pl.ds(H - R, R), cols], sem)
    cp.start()
    cp.wait()


def local_backward(act_blk, w_blk, grad_blk):
    any_spec = pl.BlockSpec(memory_space=pl.ANY)
    vmem_spec = pl.BlockSpec(memory_space=pltpu.VMEM)
    dma = pltpu.SemaphoreType.DMA
    outs = pl.pallas_call(
        kernel,
        out_shape=(
            pltpu.VMEM((H, 2 * H), BF16),
            pltpu.VMEM((H, N), F32),
            jax.ShapeDtypeStruct((2, 2, H, N), BF16),
            jax.ShapeDtypeStruct((2, 4, D, T), F32),
            jax.ShapeDtypeStruct((R, T), F32),
        ),
        in_specs=[any_spec] * 3,
        out_specs=(vmem_spec,) * 2 + (any_spec,) * 3,
        scratch_shapes=[
            pltpu.VMEM((2, 2, H, N), BF16),
            pltpu.VMEM((4, 4, D, T), F32),
            pltpu.VMEM((4, 4, D, T), F32),
            pltpu.VMEM((2, 2, T, N), BF16),
            pltpu.VMEM((2, 4, D, T), F32),
            dma, dma((4,)), dma((2, 4)), dma((4,)), dma((4,)), dma((5,)), dma((2, 8)), dma((16,)), dma((2, 8)),
            dma((4,)), dma((2, 8)), dma((2, 4)), dma((2, 4)), dma((4, 4)), dma((2, 16)),
            dma, dma, dma, dma, dma, dma, dma, dma, dma, dma((2, 2)), dma,
        ],
        compiler_params=pltpu.CompilerParams(
            collective_id=0, has_side_effects=True, vmem_limit_bytes=41_800_000
        ),
        cost_estimate=pl.CostEstimate(flops=8 * H * H * H, bytes_accessed=100 << 20, transcendentals=0),
    )(act_blk, w_blk, grad_blk)
    tail = lax.ppermute(outs[4], "row", [(i, (i + 2) % 4) for i in range(4)])
    dx, dw = pl.pallas_call(
        store_kernel,
        out_shape=(jax.ShapeDtypeStruct((H, 2 * H), BF16), jax.ShapeDtypeStruct((H, N), F32)),
        in_specs=[vmem_spec] * 2,
        out_specs=(any_spec,) * 2,
        scratch_shapes=[dma((2, 4))],
        compiler_params=pltpu.CompilerParams(vmem_limit_bytes=1 << 20),
        cost_estimate=pl.CostEstimate(flops=0, bytes_accessed=48 << 20, transcendentals=0),
    )(outs[0], outs[1])
    dw = pl.pallas_call(
        add_kernel,
        out_shape=jax.ShapeDtypeStruct((H, N), F32),
        in_specs=[any_spec] + [vmem_spec] * 2,
        out_specs=any_spec,
        scratch_shapes=[pltpu.VMEM((R, T), F32), dma],
        input_output_aliases={0: 0},
        compiler_params=pltpu.CompilerParams(vmem_limit_bytes=2 << 20),
        cost_estimate=pl.CostEstimate(flops=0, bytes_accessed=1 << 20, transcendentals=0),
    )(dw, outs[1], tail)
    return dx, dw


def solution(mesh):
    io_spec = P(("dp", "row"), "col")
    w_spec = P("row", "col")
    return jax.shard_map(
        local_backward, mesh=mesh, in_specs=(io_spec, w_spec, io_spec), out_specs=(io_spec, io_spec), check_vma=False
    )
```

time: 1470 us -> 288 us (0.20)
  waiting for transfers between devices: 1350 us -> 0.01 us
  Pallas kernels: 0 us -> 286 us
  matrix products: 87.1 us -> 0 us
  other arithmetic: 17.4 us -> 0 us
    reduce_scatter x2 -> x0, waiting for transfers between devices: 897 us -> none  [the longest x1 686 us: local_backward(): lax.psum_scatter(grad_in_part, 'col', scatter_dimension=1, tiled=True)]
    all_gather x2 -> x0, waiting for transfers between devices: 450 us -> none  [the longest x1 342 us: local_backward(): act_rows = lax.all_gather(act_blk, 'col', axis=1, tiled=True)]
    pallas_call x0 -> x3, Pallas kernels: none -> 286 us  [the longest x1 277 us: local_backward(): pl.pallas_call(kernel, out_shape=(pltpu.VMEM((H, 2 * H), BF16), pltpu.VME...]
    dot_general x2 -> x0, matrix products: 87.1 us -> none  [the longest x1 45 us: local_backward(): jnp.einsum('tn,kn->tk', grad_blk, w_cols, preferred_element_type=jnp.floa...]
    convert_element_type x1 -> x0, other arithmetic: 17.4 us -> none  [local_backward(): lax.psum_scatter(grad_in_part, 'col', scatter_dimension=1, tiled=True)]
  transfers between devices with their start and end apart: 4 -> 1, of which waited for: 4 -> 0; matrix products, arithmetic and copies ran while one was open for 7% -> 0% of each run, Pallas kernels for 0% -> 3%
where the time goes in v6:
time: 288 us
  Pallas kernels  286 us (99%)
    pallas_call x1, Pallas kernels, local_backward(): pl.pallas_call(kernel, out_shape=(pltpu.VMEM((H, 2 * H), BF16), pltpu.VME...  277 us
    pallas_call x1, Pallas kernels, local_backward(): pl.pallas_call(store_kernel, out_shape=(jax.ShapeDtypeStruct((H, 2 * H),...  8.44 us
  transfers between devices with their start and end apart: 1, of which 0 were waited for; matrix products, arithmetic and copies ran while one was open for 0% of the time, Pallas kernels for 3%

profile of v6, /device:TPU:0, one launch (start us, length us, event | category | flops | bytes accessed | tf_op | source)
XLA Modules:
  0.0 287.7 jit_solution(9561046863576312930)
XLA Ops:
  0.6 277.0 %shard_map.50 = (bf16[2048,4096]{1,0:T(8,128)(2,1)S(1)}, f32[2048,1024]{1,0:T(8,128)S(1)}, bf16[2,2,2048,1024]{3,2,1,0:T(8,128)(2,1)}, f32[2,4,512,256]{3,2,1,0:T(8,128)}, f32[320,256]{1,0:T(8,128)}) custom-call(bf16[2048,4096]{1,0:T(8,128)(2,1)} %x_ref.1, bf16[2048,1024]{1,0:T(8,128)(2,1)} %w_ref.1, bf16[2048,1024]{1,0:T(8,128)(2,1)} %dy_ref.1), custom_call_target="tpu_custom_call" | custom-call | flops 68719476736 | bytes 104857600 | tf_op jit(solution)/shard_map/pallas_call | solution.py:555
  277.6 0.7 collective-permute-start
  278.3 8.4 %shard_map.51 = (bf16[2048,4096]{1,0:T(8,128)(2,1)}, f32[2048,1024]{1,0:T(8,128)}) custom-call(bf16[2048,4096]{1,0:T(8,128)(2,1)S(1)} %get-tuple-element.7.dx_ref, f32[2048,1024]{1,0:T(8,128)S(1)} %get-tuple-element.8.dw_ref), custom_call_target="tpu_custom_call" | custom-call | bytes 50331648 | tf_op jit(solution)/shard_map/pallas_call | solution.py:582
  286.7 0.0 collective-permute-done.tail_ref
  286.8 0.8 shard_map.52
Async XLA Ops:
  277.6 9.1 %collective-permute-start = (f32[320,256]{1,0:T(8,128)}, f32[320,256]{1,0:T(8,128)S(1)}, u32[]{:S(2)}, u32[]{:S(2)}) collective-permute-start(f32[320,256]{1,0:T(8,128)} %get-tuple-element.11), channel_id=1, source_target_pairs={{0,2},{1,3},{2,0},{3,1},{4,6},{5,7},{6,4},{7,5}} | collective-permute-start | bytes 983048 | tf_op jit(solution)/shard_map/ppermute | solution.py:581

commit v7 on v6

--- a/solution.py
+++ b/solution.py
@@ -9,7 +9,9 @@
 F32 = jnp.float32
 BF16 = jnp.bfloat16
 H, N, D, T, Q, S = 2048, 1024, 512, 256, 128, 64
-R = 320
+R = 352
+E = 96
+F = D - E - R
 ME, SIB = 0, 1
 OWN, OTH = 0, 1
 ARG, BUF = "arg", "buf"
@@ -38,10 +40,10 @@
 
 def kernel(
     x_ref, w_ref, dy_ref,
-    dx_ref, dw_ref, wbuf, bufy, tail,
-    dyv, pown, poth, wv, land,
+    dx_ref, dw_ref, wbuf, bufy, tail, tail_y,
+    dyv, pown, poth, wv, land, extra,
     dy_sem, x_sem, dys_r, dyy_r, xs_r, xf_r, w_r, wp_r, ws_r, pa_r, ph_r, po_r, ps_r, py_r, pf_r,
-    s_dys, s_dyy, s_xs, s_w, s_ws, s_px, s_po, s_py, s_sum, wl_sem, tail_sem,
+    s_dys, s_dyy, s_xs, s_w, s_ws, s_px, s_po, s_py, s_sum, wl_sem, tail_sem, tail_y_sem, s_ex, ex_r, py_ex,
 ):
     row = lax.axis_index("row")
     y = lax.axis_index("col")
@@ -159,18 +161,35 @@
         return remote(bufy.at[q, kt, part], land.at[q, kt, part], s_px, pf_r.at[q, 4 * kt + r], xn)
 
     def p_trans_short():
-        part = pl.ds(Q, S)
-        return remote(poth.at[1, 3, part], bufy.at[1, 3, part], s_py, pf_r.at[1, 13], yn)
+        part = pl.ds(0, F)
+        return remote(poth.at[1, 3, part], bufy.at[1, 3, part], s_py, pf_r.at[1, 12], yn)
 
     def p_fwd_short():
-        part = pl.ds(Q, S)
-        return remote(bufy.at[1, 3, part], land.at[1, 3, part], s_px, pf_r.at[1, 13], xn)
+        part = pl.ds(0, F)
+        return remote(bufy.at[1, 3, part], land.at[1, 3, part], s_px, pf_r.at[1, 12], xn)
 
     def p_trans_tail():
-        return remote(poth.at[1, 3, pl.ds(D - R, R)], tail, s_py, pf_r.at[1, 14], yn)
+        return remote(poth.at[1, 3, pl.ds(F, R)], tail, s_py, pf_r.at[1, 13], yn)
+
+    def p_extra():
+        return remote(poth.at[1, 3, pl.ds(D - E, E)], extra, s_ex, ex_r, xn)
+
+    def extra_to_y():
+        return remote(poth.at[1, 3, pl.ds(D - E, E)], dw_part(1, 4 * D - E, E), s_py, py_ex, yn)
 
     def p_term(q, kt):
         return remote(poth.at[q, kt], dw_tile(q, kt), s_py, py_r.at[q, kt], yn)
+
+    def p_term_short():
+        part = pl.ds(0, D - E)
+        return remote(poth.at[1, 3, part], dw_part(1, 3 * D, D - E), s_py, py_r.at[1, 3], yn)
+
+    def sum_short():
+        part = pl.ds(0, D - E)
+        return remote(poth.at[3, 3, part], dw_part(3, 3 * D, D - E), s_sum, py_r.at[3, 3], yn)
+
+    def tail_y_store(src):
+        return local(src.at[3, 3, pl.ds(D - E, E)], tail_y, tail_y_sem)
 
     def sum_to_y(q, kt):
         return remote(poth.at[q, kt], dw_tile(q, kt), s_sum, py_r.at[q, kt], yn)
@@ -272,17 +291,17 @@
             for r in range(4):
                 p_trans(q, kt, r).start()
             return
-        p_trans(q, kt, 0).start()
 
         @pl.when(kt < 3)
         def _():
-            for r in (1, 2, 3):
+            for r in range(4):
                 p_trans(q, kt, r).start()
 
         @pl.when(kt == 3)
         def _():
             p_trans_short().start()
             p_trans_tail().start()
+            p_extra().start()
 
     def dy_in(q):
         dy_to_y(q).wait_recv()
@@ -295,9 +314,13 @@
         def tile(kt):
             p_tile(poth, OTH, q, kt)
             if q < 2:
-                @pl.when(is_a)
+                @pl.when(jnp.logical_and(is_a, 4 * q + kt < 7))
                 def _():
                     p_term(q, kt).start()
+
+                @pl.when(jnp.logical_and(is_a, 4 * q + kt == 7))
+                def _():
+                    p_term_short().start()
 
                 @pl.when(is_b)
                 def _():
@@ -370,7 +393,15 @@
         def a_sum(q, kt):
             p_other(q, kt).wait_recv()
             poth[q, kt] = poth[q, kt] + land[q - 2, kt]
-            sum_to_y(q, kt).start()
+
+            @pl.when(4 * q + kt < 15)
+            def _():
+                sum_to_y(q, kt).start()
+
+            @pl.when(4 * q + kt == 15)
+            def _():
+                sum_short().start()
+                tail_y_store(poth).start()
 
         def early(i):
             w_to_y(i).wait_recv()
@@ -387,6 +418,9 @@
             final_early(4 + kt)
 
         loop(4, q2_tile)
+        p_extra().wait_recv()
+        poth[1, 3, D - E:] = poth[1, 3, D - E:] + extra[...]
+        extra_to_y().start()
         start_loads(0, ME, ARG)
         dy_in(3)
 
@@ -448,7 +482,7 @@
             def _():
                 final_late((i - 26) // 4)
 
-        loop(45, step)
+        loop(44, step)
         p_trans_short().wait_recv()
         p_fwd_short().start()
         low = dw_part(3, 4 * D - R, R)
@@ -460,9 +494,10 @@
         top = dw_part(3, 3 * D, D - R)
         top[...] = top[...] + pown[3, 3, :D - R]
         drain(wbuf.at[ME], s_w)
-        drain(dyv.at[ME, OWN, pl.ds(0, H - R // 2)], s_px)
+        tail_y_store(poth).wait()
+        drain(dyv.at[ME, OWN, pl.ds(0, H - (E + R) // 2)], s_px)
         drain(land, s_py)
-        drain(land, s_sum)
+        drain(dyv.at[ME, OWN, pl.ds(0, H - E // 2)], s_sum)
 
     @pl.when(is_b)
     def _():
@@ -472,6 +507,7 @@
             p_own(2 + t // 4, t % 4).start()
         p_own_last().start()
         tail_store().start()
+        tail_y_store(pown).start()
 
         def own_w(i):
             w_own_to_x(i).wait_recv()
@@ -508,18 +544,22 @@
             tile = dw_part(q, kt * D + r * Q, Q)
             tile[...] = tile[...] + land[q, kt, pl.ds(r * Q, Q)]
 
-        loop(29, fin)
+        loop(28, fin)
+        p_term_short().wait_recv()
         p_fwd_short().wait_recv()
-        tile = dw_part(1, 3 * D + Q, S)
-        tile[...] = tile[...] + land[1, 3, Q:Q + S]
-        for q in (2, 3):
-            for kt in range(4):
-                sum_to_y(q, kt).wait_recv()
+        tile = dw_part(1, 3 * D, F)
+        tile[...] = tile[...] + land[1, 3, :F]
+        extra_to_y().wait_recv()
+        for t in range(7):
+            sum_to_y(2 + t // 4, t % 4).wait_recv()
+        sum_short().wait_recv()
+        tail_y_store(pown).wait()
         tail_store().wait()
         drain(wbuf.at[ME, OWN], s_w)
         drain(dw_ref.at[pl.ds(0, H - R // 4)], s_px)
         drain(land, s_po)
-        drain(land, s_py)
+        drain(extra, s_ex)
+        drain(dyv.at[ME, OWN, pl.ds(0, H - E // 2)], s_py)
 
     drain(dyv.at[ME], s_dys)
     drain(dyv.at[ME, OWN], s_dyy)
@@ -539,13 +579,19 @@
         cp.wait()
 
 
-def add_kernel(done_ref, dw_ref, tail_ref, dw_out, buf, sem):
+def add_kernel(done_ref, dw_ref, tail_ref, tail_y_ref, dw_out, buf, buf_y, sem, sem_y):
     is_a = lax.axis_index("row") // 2 == lax.axis_index("col")
+    rows = cut(jnp.where(is_a, H - R, 3 * D + F), R, 32)
     cols = cut(jnp.where(is_a, 3 * T, T), T)
-    buf[...] = dw_ref[H - R:, cols] + tail_ref[...]
-    cp = pltpu.make_async_copy(buf, dw_out.at[pl.ds(H - R, R), cols], sem)
-    cp.start()
-    cp.wait()
+    buf[...] = dw_ref[rows, cols] + tail_ref[...]
+    first = pltpu.make_async_copy(buf, dw_out.at[rows, cols], sem)
+    first.start()
+    rows_y, cols_y = pl.ds(H - E, E), cut(jnp.where(is_a, 0, 3 * T), T)
+    buf_y[...] = jnp.where(is_a, dw_ref[rows_y, cols_y], tail_y_ref[...])
+    second = pltpu.make_async_copy(buf_y, dw_out.at[rows_y, cols_y], sem_y)
+    second.start()
+    first.wait()
+    second.wait()
 
 
 def local_backward(act_blk, w_blk, grad_blk):
@@ -560,18 +606,21 @@
             jax.ShapeDtypeStruct((2, 2, H, N), BF16),
             jax.ShapeDtypeStruct((2, 4, D, T), F32),
             jax.ShapeDtypeStruct((R, T), F32),
+            jax.ShapeDtypeStruct((E, T), F32),
         ),
         in_specs=[any_spec] * 3,
-        out_specs=(vmem_spec,) * 2 + (any_spec,) * 3,
+        out_specs=(vmem_spec,) * 2 + (any_spec,) * 4,
         scratch_shapes=[
             pltpu.VMEM((2, 2, H, N), BF16),
             pltpu.VMEM((4, 4, D, T), F32),
             pltpu.VMEM((4, 4, D, T), F32),
             pltpu.VMEM((2, 2, T, N), BF16),
             pltpu.VMEM((2, 4, D, T), F32),
+            pltpu.VMEM((E, T), F32),
             dma, dma((4,)), dma((2, 4)), dma((4,)), dma((4,)), dma((5,)), dma((2, 8)), dma((16,)), dma((2, 8)),
             dma((4,)), dma((2, 8)), dma((2, 4)), dma((2, 4)), dma((4, 4)), dma((2, 16)),
             dma, dma, dma, dma, dma, dma, dma, dma, dma, dma((2, 2)), dma,
+            dma, dma, dma, dma,
         ],
         compiler_params=pltpu.CompilerParams(
             collective_id=0, has_side_effects=True, vmem_limit_bytes=41_800_000
@@ -579,6 +628,7 @@
         cost_estimate=pl.CostEstimate(flops=8 * H * H * H, bytes_accessed=100 << 20, transcendentals=0),
     )(act_blk, w_blk, grad_blk)
     tail = lax.ppermute(outs[4], "row", [(i, (i + 2) % 4) for i in range(4)])
+    tail_y = lax.ppermute(outs[5], "col", [(0, 1), (1, 0)])
     dx, dw = pl.pallas_call(
         store_kernel,
         out_shape=(jax.ShapeDtypeStruct((H, 2 * H), BF16), jax.ShapeDtypeStruct((H, N), F32)),
@@ -591,13 +641,13 @@
     dw = pl.pallas_call(
         add_kernel,
         out_shape=jax.ShapeDtypeStruct((H, N), F32),
-        in_specs=[any_spec] + [vmem_spec] * 2,
+        in_specs=[any_spec] + [vmem_spec] * 3,
         out_specs=any_spec,
-        scratch_shapes=[pltpu.VMEM((R, T), F32), dma],
+        scratch_shapes=[pltpu.VMEM((R, T), F32), pltpu.VMEM((E, T), F32), dma, dma],
         input_output_aliases={0: 0},
         compiler_params=pltpu.CompilerParams(vmem_limit_bytes=2 << 20),
         cost_estimate=pl.CostEstimate(flops=0, bytes_accessed=1 << 20, transcendentals=0),
-    )(dw, outs[1], tail)
+    )(dw, outs[1], tail, tail_y)
     return dx, dw
 
 

time: 288 us -> 288 us (level)
  transfers between devices with their start and end apart: 1 -> 2, of which waited for: 0 -> 0; matrix products, arithmetic and copies ran while one was open for 0% -> 0% of each run, Pallas kernels for 3% -> 3%
where the time goes in v7:
time: 288 us; the launch traced here: 287 us
  Pallas kernels  284 us (99%)
    pallas_call x1, Pallas kernels, local_backward(): pl.pallas_call(kernel, out_shape=(pltpu.VMEM((H, 2 * H), BF16), pltpu.VME...  275 us
    pallas_call x1, Pallas kernels, local_backward(): pl.pallas_call(store_kernel, out_shape=(jax.ShapeDtypeStruct((H, 2 * H),...  8.44 us
  transfers between devices with their start and end apart: 2, of which 0 were waited for; matrix products, arithmetic and copies ran while one was open for 0% of the time, Pallas kernels for 3%

profile of v7, /device:TPU:0, one launch (start us, length us, event | category | flops | bytes accessed | tf_op | source)
XLA Modules:
  0.0 287.3 jit_solution(15166760747434757763)
XLA Ops:
  0.6 275.1 %shard_map.50 = (bf16[2048,4096]{1,0:T(8,128)(2,1)S(1)}, f32[2048,1024]{1,0:T(8,128)S(1)}, bf16[2,2,2048,1024]{3,2,1,0:T(8,128)(2,1)}, f32[2,4,512,256]{3,2,1,0:...) custom-call(bf16[2048,4096]{1,0:T(8,128)(2,1)} %x_ref.1, bf16[2048,1024]{1,0:T(8,128)(2,1)} %w_ref.1, ...), custom_call_target="tpu_custom_call" | custom-call | flops 68719476736 | bytes 104857600 | tf_op jit(solution)/shard_map/pallas_call | solution.py:601
  275.8 0.5 collective-permute-start
  276.2 1.6 collective-permute-start.1
  277.8 8.4 %shard_map.51 = (bf16[2048,4096]{1,0:T(8,128)(2,1)}, f32[2048,1024]{1,0:T(8,128)}) custom-call(bf16[2048,4096]{1,0:T(8,128)(2,1)S(1)} %get-tuple-element.8.dx_ref, f32[2048,1024]{1,0:T(8,128)S(1)} %get-tuple-element.9.dw_ref), custom_call_target="tpu_custom_call" | custom-call | bytes 50331648 | tf_op jit(solution)/shard_map/pallas_call | solution.py:632
  286.3 0.0 collective-permute-done.1.tail_y_ref
  286.3 0.0 collective-permute-done.tail_ref
  286.3 0.8 shard_map.52
Async XLA Ops:
  275.8 10.5 %collective-permute-start = (f32[352,256]{1,0:T(8,128)}, f32[352,256]{1,0:T(8,128)S(1)}, u32[]{:S(2)}, u32[]{:S(2)}) collective-permute-start(f32[352,256]{1,0:T(8,128)} %get-tuple-element.12), channel_id=1, source_target_pairs={{0,2},{1,3},{2,0},{3,1},{4,6},{5,7},{6,4},{7,5}} | collective-permute-start | bytes 1081352 | tf_op jit(solution)/shard_map/ppermute | solution.py:630
  276.2 10.0 %collective-permute-start.1 = (f32[96,256]{1,0:T(8,128)}, f32[96,256]{1,0:T(8,128)S(1)}, u32[]{:S(2)}, u32[]{:S(2)}) collective-permute-start(f32[96,256]{1,0:T(8,128)} %get-tuple-element.13), channel_id=1, source_target_pairs={{0,4},{4,0},{1,5},{5,1},{2,6},{6,2},{3,7},{7,3}} | collective-permute-start | bytes 294920 | tf_op jit(solution)/shard_map/ppermute | solution.py:631

commit v8 on v7

--- a/solution.py
+++ b/solution.py
@@ -10,7 +10,7 @@
 BF16 = jnp.bfloat16
 H, N, D, T, Q, S = 2048, 1024, 512, 256, 128, 64
 R = 352
-E = 96
+E = 128
 F = D - E - R
 ME, SIB = 0, 1
 OWN, OTH = 0, 1
@@ -43,7 +43,7 @@
     dx_ref, dw_ref, wbuf, bufy, tail, tail_y,
     dyv, pown, poth, wv, land, extra,
     dy_sem, x_sem, dys_r, dyy_r, xs_r, xf_r, w_r, wp_r, ws_r, pa_r, ph_r, po_r, ps_r, py_r, pf_r,
-    s_dys, s_dyy, s_xs, s_w, s_ws, s_px, s_po, s_py, s_sum, wl_sem, tail_sem, tail_y_sem, s_ex, ex_r, py_ex,
+    s_dys, s_dyy, s_xs, s_w, s_ws, s_px, s_po, s_py, s_sum, wl_sem, tail_sem, tail_y_sem, s_ex, ex_r, py_ex, dyq_sem, xt_sem, s_x0,
 ):
     row = lax.axis_index("row")
     y = lax.axis_index("col")
@@ -78,7 +78,10 @@
     def dw_tile(q, kt):
         return dw_part(q, kt * D, D)
 
-    dy_load = local(dy_ref, dyv.at[ME, OWN], dy_sem)
+    dyq_load = local(dy_ref.at[:, pl.ds(0, T)], dyv.at[ME, OWN, :, pl.ds(0, T)], dyq_sem)
+    dy_load = local(dy_ref.at[:, pl.ds(T, N - T)], dyv.at[ME, OWN, :, pl.ds(T, N - T)], dy_sem)
+    xt_load = local(x_ref.at[:, pl.ds((1 - c) * H, Q)], xo(3 * D, Q), xt_sem)
+    x_first_piece = remote(xo(3 * D, Q), xs(0, Q), s_x0, xf_r.at[0], sib)
 
     def x_load(kt):
         return local(x_ref.at[:, pl.ds(c * H + kt * D, D)], xo(kt * D, D), x_sem.at[kt])
@@ -90,12 +93,13 @@
         return x_cols_to_sib(kt * D, D, xs_r.at[kt])
 
     def x_first(i):
-        k0, n = ((0, Q), (Q, Q), (T, T))[i]
-        return x_cols_to_sib(k0, n, xf_r.at[i])
+        if i == 0:
+            return x_first_piece
+        return x_cols_to_sib(i * Q, i * Q, xf_r.at[i])
 
     def dy_first(i):
         cols = pl.ds(i * Q, Q)
-        return remote(dy_ref.at[:, cols], dyv.at[SIB, OWN, :, cols], s_dys, xf_r.at[3 + i], sib)
+        return remote(dyv.at[ME, OWN, :, cols], dyv.at[SIB, OWN, :, cols], s_dys, xf_r.at[3 + i], sib)
 
     def dy_to_sib(j, q):
         src = dy_ref.at[:, qs(q)] if j == OWN else dyv.at[ME, OTH, :, qs(q)]
@@ -197,18 +201,24 @@
     def drain(ref, sem):
         remote(ref, ref, sem, dyy_r.at[0], yn).wait_send()
 
-    dy_load.start()
-    for kt in range(4):
-        x_load(kt).start()
+    for cp in (dyq_load, xt_load, x_load(0), dy_load, x_load(1), x_load(2)):
+        cp.start()
 
     barrier = pltpu.get_barrier_semaphore()
     for dev in (sib, xn, yn):
         pl.semaphore_signal(barrier, inc=1, device_id=dev, device_id_type=MESH)
     pl.semaphore_wait(barrier, 3)
 
+    dy_to_y(0).start()
+
+    @pl.when(is_a)
+    def _():
+        w_own_to_x(0).start()
+
+    dyq_load.wait()
     dy_first(0).start()
+    xt_load.wait()
     x_first(0).start()
-    dy_to_y(0).start()
     dy_first(1).start()
     x_first(1).start()
     x_first(2).start()
@@ -216,7 +226,7 @@
 
     @pl.when(is_a)
     def _():
-        for i in range(8):
+        for i in range(1, 8):
             w_own_to_x(i).start()
         for q in (2, 3):
             dy_to_y(q).start()
@@ -256,7 +266,6 @@
     def put(ref, value):
         ref[...] = value
 
-    dy_load.wait()
     x_load(0).wait()
     dy_first(0).wait_recv()
     for i, (r0, n, c0, m) in enumerate(FIRST):
@@ -269,6 +278,10 @@
         @pl.when(is_b)
         def _(i=i):
             p_first(i).start()
+
+    x_first(0).wait_send()
+    x_load(3).start()
+    dy_load.wait()
 
     def own_tile(q, kt):
         if q == 0:
@@ -563,7 +576,7 @@
 
     drain(dyv.at[ME], s_dys)
     drain(dyv.at[ME, OWN], s_dyy)
-    drain(wbuf.at[ME], s_xs)
+    drain(dx_ref.at[:, pl.ds(0, H - Q)], s_xs)
     drain(wbuf.at[ME], s_ws)
 
 
@@ -620,7 +633,7 @@
             dma, dma((4,)), dma((2, 4)), dma((4,)), dma((4,)), dma((5,)), dma((2, 8)), dma((16,)), dma((2, 8)),
             dma((4,)), dma((2, 8)), dma((2, 4)), dma((2, 4)), dma((4, 4)), dma((2, 16)),
             dma, dma, dma, dma, dma, dma, dma, dma, dma, dma((2, 2)), dma,
-            dma, dma, dma, dma,
+            dma, dma, dma, dma, dma, dma, dma,
         ],
         compiler_params=pltpu.CompilerParams(
             collective_id=0, has_side_effects=True, vmem_limit_bytes=41_800_000

time: 288 us -> 289 us (level)
  transfers between devices with their start and end apart: 2 -> 2, of which waited for: 0 -> 1; matrix products, arithmetic and copies ran while one was open for 0% -> 0% of each run, Pallas kernels for 3% -> 3%
where the time goes in v8:
time: 289 us; the launch traced here: 288 us
  Pallas kernels  285 us (99%)
    pallas_call x1, Pallas kernels, local_backward(): pl.pallas_call(kernel, out_shape=(pltpu.VMEM((H, 2 * H), BF16), pltpu.VME...  276 us
    pallas_call x1, Pallas kernels, local_backward(): pl.pallas_call(store_kernel, out_shape=(jax.ShapeDtypeStruct((H, 2 * H),...  8.44 us
  transfers between devices with their start and end apart: 2, of which 1 were waited for; matrix products, arithmetic and copies ran while one was open for 0% of the time, Pallas kernels for 3%

profile of v8, /device:TPU:0, one launch (start us, length us, event | category | flops | bytes accessed | tf_op | source)
XLA Modules:
  0.0 288.4 jit_solution(11586949652800164950)
XLA Ops:
  0.6 276.2 %shard_map.50 = (bf16[2048,4096]{1,0:T(8,128)(2,1)S(1)}, f32[2048,1024]{1,0:T(8,128)S(1)}, bf16[2,2,2048,1024]{3,2,1,0:T(8,128)(2,1)}, f32[2,4,512,256]{3,2,1,0:...) custom-call(bf16[2048,4096]{1,0:T(8,128)(2,1)} %x_ref.1, bf16[2048,1024]{1,0:T(8,128)(2,1)} %w_ref.1, ...), custom_call_target="tpu_custom_call" | custom-call | flops 68719476736 | bytes 104857600 | tf_op jit(solution)/shard_map/pallas_call | solution.py:614
  276.8 0.0 collective-permute-start
  276.8 2.0 collective-permute-start.1
  278.9 8.4 %shard_map.51 = (bf16[2048,4096]{1,0:T(8,128)(2,1)}, f32[2048,1024]{1,0:T(8,128)}) custom-call(bf16[2048,4096]{1,0:T(8,128)(2,1)S(1)} %get-tuple-element.8.dx_ref, f32[2048,1024]{1,0:T(8,128)S(1)} %get-tuple-element.9.dw_ref), custom_call_target="tpu_custom_call" | custom-call | bytes 50331648 | tf_op jit(solution)/shard_map/pallas_call | solution.py:645
  287.3 0.0 collective-permute-done.1.tail_y_ref
  287.3 0.1 collective-permute-done.tail_ref
  287.4 0.8 shard_map.52
Async XLA Ops:
  276.8 10.6 %collective-permute-start = (f32[352,256]{1,0:T(8,128)}, f32[352,256]{1,0:T(8,128)S(1)}, u32[]{:S(2)}, u32[]{:S(2)}) collective-permute-start(f32[352,256]{1,0:T(8,128)} %get-tuple-element.12), channel_id=1, source_target_pairs={{0,2},{1,3},{2,0},{3,1},{4,6},{5,7},{6,4},{7,5}} | collective-permute-start | bytes 1081352 | tf_op jit(solution)/shard_map/ppermute | solution.py:643
  276.8 10.5 %collective-permute-start.1 = (f32[128,256]{1,0:T(8,128)}, f32[128,256]{1,0:T(8,128)S(1)}, u32[]{:S(2)}, u32[]{:S(2)}) collective-permute-start(f32[128,256]{1,0:T(8,128)} %get-tuple-element.13), channel_id=1, source_target_pairs={{0,4},{4,0},{1,5},{5,1},{2,6},{6,2},{3,7},{7,3}} | collective-permute-start | bytes 393224 | tf_op jit(solution)/shard_map/ppermute | solution.py:644

commit v9 on v7

--- a/solution.py
+++ b/solution.py
@@ -10,12 +10,12 @@
 BF16 = jnp.bfloat16
 H, N, D, T, Q, S = 2048, 1024, 512, 256, 128, 64
 R = 352
-E = 96
+E = 128
 F = D - E - R
 ME, SIB = 0, 1
 OWN, OTH = 0, 1
 ARG, BUF = "arg", "buf"
-FIRST = ((0, Q, 0, Q), (0, Q, Q, Q), (Q, Q, 0, T), (T, T, 0, T))
+FIRST = ((0, T), (T, T))
 
 
 def _tdot(a, b):
@@ -41,9 +41,9 @@
 def kernel(
     x_ref, w_ref, dy_ref,
     dx_ref, dw_ref, wbuf, bufy, tail, tail_y,
-    dyv, pown, poth, wv, land, extra,
+    dyv, pown, poth, wv, land, extra, swap,
     dy_sem, x_sem, dys_r, dyy_r, xs_r, xf_r, w_r, wp_r, ws_r, pa_r, ph_r, po_r, ps_r, py_r, pf_r,
-    s_dys, s_dyy, s_xs, s_w, s_ws, s_px, s_po, s_py, s_sum, wl_sem, tail_sem, tail_y_sem, s_ex, ex_r, py_ex,
+    s_dys, s_dyy, s_xs, s_w, s_ws, s_px, s_po, s_py, s_sum, wl_sem, tail_sem, tail_y_sem, s_ex, ex_r, py_ex, dyq_sem, xt_sem, xq_sem, s_sw, sw_r,
 ):
     row = lax.axis_index("row")
     y = lax.axis_index("col")
@@ -78,7 +78,12 @@
     def dw_tile(q, kt):
         return dw_part(q, kt * D, D)
 
-    dy_load = local(dy_ref, dyv.at[ME, OWN], dy_sem)
+    dyq_load = local(dy_ref.at[:, pl.ds(0, T)], dyv.at[ME, OWN, :, pl.ds(0, T)], dyq_sem)
+    dy_load = local(dy_ref.at[:, pl.ds(T, N - T)], dyv.at[ME, OWN, :, pl.ds(T, N - T)], dy_sem)
+    xt_load = local(x_ref.at[:, pl.ds((1 - c) * H, T)], xo(3 * D, T), xt_sem)
+    xq_load = local(x_ref.at[:, pl.ds(c * H, T)], xo(0, T), xq_sem)
+    x0_load = local(x_ref.at[:, pl.ds(c * H + T, D - T)], xo(T, D - T), x_sem.at[0])
+    swap_part = remote(swap.at[0], swap.at[1], s_sw, sw_r, sib)
 
     def x_load(kt):
         return local(x_ref.at[:, pl.ds(c * H + kt * D, D)], xo(kt * D, D), x_sem.at[kt])
@@ -90,12 +95,8 @@
         return x_cols_to_sib(kt * D, D, xs_r.at[kt])
 
     def x_first(i):
-        k0, n = ((0, Q), (Q, Q), (T, T))[i]
+        k0, n = FIRST[i]
         return x_cols_to_sib(k0, n, xf_r.at[i])
-
-    def dy_first(i):
-        cols = pl.ds(i * Q, Q)
-        return remote(dy_ref.at[:, cols], dyv.at[SIB, OWN, :, cols], s_dys, xf_r.at[3 + i], sib)
 
     def dy_to_sib(j, q):
         src = dy_ref.at[:, qs(q)] if j == OWN else dyv.at[ME, OTH, :, qs(q)]
@@ -127,11 +128,8 @@
         return remote(ref, wbuf.at[SIB, j, qs(i)], s_ws, ws_r.at[j, i], sib)
 
     def p_first(i):
-        r0, n, c0, m = FIRST[i]
-        return remote(
-            pown.at[0, 0, pl.ds(r0, n), pl.ds(c0, m)], dw_ref.at[pl.ds(r0, n), pl.ds(c0, m)],
-            s_px, pa_r.at[i], xn,
-        )
+        r0, n = FIRST[i]
+        return remote(pown.at[0, 0, pl.ds(r0, n)], dw_part(0, r0, n), s_px, pa_r.at[i], xn)
 
     def p_half(q, kt, h):
         return remote(
@@ -197,21 +195,15 @@
     def drain(ref, sem):
         remote(ref, ref, sem, dyy_r.at[0], yn).wait_send()
 
-    dy_load.start()
-    for kt in range(4):
-        x_load(kt).start()
+    for cp in (dyq_load, xt_load, xq_load):
+        cp.start()
 
     barrier = pltpu.get_barrier_semaphore()
     for dev in (sib, xn, yn):
         pl.semaphore_signal(barrier, inc=1, device_id=dev, device_id_type=MESH)
     pl.semaphore_wait(barrier, 3)
 
-    dy_first(0).start()
-    x_first(0).start()
     dy_to_y(0).start()
-    dy_first(1).start()
-    x_first(1).start()
-    x_first(2).start()
     dy_to_y(1).start()
 
     @pl.when(is_a)
@@ -230,6 +222,17 @@
         for p in range(16):
             w_to_y_piece(p).start()
 
+    dyq_load.wait()
+    xt_load.wait()
+    xq_load.wait()
+    swap[0] = _tdot(dx_ref[:, 3 * D:3 * D + T], dyv[ME, OWN, :, :T])
+    swap_part.start()
+    dy_to_sib(OWN, 0).start()
+    x_first(1).start()
+    pown[0, 0, :T] = _tdot(dx_ref[:, :T], dyv[ME, OWN, :, :T])
+    for cp in (x0_load, dy_load, x_load(1), x_load(2), x_load(3)):
+        cp.start()
+    x_first(0).start()
     for kt in (1, 2, 3):
         x_to_sib(kt).start()
     for q in (1, 2, 3):
@@ -240,8 +243,15 @@
         for i in range(8):
             w_to_sib(OWN, i, ARG).start()
 
-    def p_part(j, c0, k0, n, m=T):
-        dy = pl.ds(c0, m)
+    swap_part.wait_recv()
+    pown[0, 0, :T] = pown[0, 0, :T] + swap[1]
+
+    @pl.when(is_b)
+    def _():
+        p_first(0).start()
+
+    def p_part(j, c0, k0, n):
+        dy = pl.ds(c0, T)
         acc = None
         for t in range(2):
             part = pl.ds(t * N, N)
@@ -256,19 +266,17 @@
     def put(ref, value):
         ref[...] = value
 
+    x0_load.wait()
+    dy_to_sib(OWN, 0).wait_recv()
+    x_first(1).wait_recv()
+    pown[0, 0, T:] = p_part(OWN, 0, T, T)
+
+    @pl.when(is_b)
+    def _():
+        p_first(1).start()
+
+    x_first(0).wait_recv()
     dy_load.wait()
-    x_load(0).wait()
-    dy_first(0).wait_recv()
-    for i, (r0, n, c0, m) in enumerate(FIRST):
-        if i == 1:
-            dy_first(1).wait_recv()
-        else:
-            x_first(max(i - 1, 0)).wait_recv()
-        put(pown.at[0, 0, pl.ds(r0, n), pl.ds(c0, m)], p_part(OWN, c0, r0, n, m))
-
-        @pl.when(is_b)
-        def _(i=i):
-            p_first(i).start()
 
     def own_tile(q, kt):
         if q == 0:
@@ -564,6 +572,7 @@
     drain(dyv.at[ME], s_dys)
     drain(dyv.at[ME, OWN], s_dyy)
     drain(wbuf.at[ME], s_xs)
+    drain(swap.at[0], s_sw)
     drain(wbuf.at[ME], s_ws)
 
 
@@ -617,10 +626,11 @@
             pltpu.VMEM((2, 2, T, N), BF16),
             pltpu.VMEM((2, 4, D, T), F32),
             pltpu.VMEM((E, T), F32),
+            pltpu.VMEM((2, T, T), F32),
             dma, dma((4,)), dma((2, 4)), dma((4,)), dma((4,)), dma((5,)), dma((2, 8)), dma((16,)), dma((2, 8)),
             dma((4,)), dma((2, 8)), dma((2, 4)), dma((2, 4)), dma((4, 4)), dma((2, 16)),
             dma, dma, dma, dma, dma, dma, dma, dma, dma, dma((2, 2)), dma,
-            dma, dma, dma, dma,
+            dma, dma, dma, dma, dma, dma, dma, dma, dma,
         ],
         compiler_params=pltpu.CompilerParams(
             collective_id=0, has_side_effects=True, vmem_limit_bytes=41_800_000

time: 288 us -> 287 us (level)
  transfers between devices with their start and end apart: 2 -> 2, of which waited for: 0 -> 1; matrix products, arithmetic and copies ran while one was open for 0% -> 0% of each run, Pallas kernels for 3% -> 3%
where the time goes in v9:
time: 287 us
  Pallas kernels  284 us (99%)
    pallas_call x1, Pallas kernels, local_backward(): pl.pallas_call(kernel, out_shape=(pltpu.VMEM((H, 2 * H), BF16), pltpu.VME...  275 us
    pallas_call x1, Pallas kernels, local_backward(): pl.pallas_call(store_kernel, out_shape=(jax.ShapeDtypeStruct((H, 2 * H),...  8.44 us
  transfers between devices with their start and end apart: 2, of which 1 were waited for; matrix products, arithmetic and copies ran while one was open for 0% of the time, Pallas kernels for 3%

profile of v9, /device:TPU:0, one launch (start us, length us, event | category | flops | bytes accessed | tf_op | source)
XLA Modules:
  0.0 286.9 jit_solution(14371823233658385620)
XLA Ops:
  0.6 274.8 %shard_map.50 = (bf16[2048,4096]{1,0:T(8,128)(2,1)S(1)}, f32[2048,1024]{1,0:T(8,128)S(1)}, bf16[2,2,2048,1024]{3,2,1,0:T(8,128)(2,1)}, f32[2,4,512,256]{3,2,1,0:...) custom-call(bf16[2048,4096]{1,0:T(8,128)(2,1)} %x_ref.1, bf16[2048,1024]{1,0:T(8,128)(2,1)} %w_ref.1, ...), custom_call_target="tpu_custom_call" | custom-call | flops 68719476736 | bytes 104857600 | tf_op jit(solution)/shard_map/pallas_call | solution.py:610
  275.4 0.1 collective-permute-start
  275.6 1.9 collective-permute-start.1
  277.5 8.4 %shard_map.51 = (bf16[2048,4096]{1,0:T(8,128)(2,1)}, f32[2048,1024]{1,0:T(8,128)}) custom-call(bf16[2048,4096]{1,0:T(8,128)(2,1)S(1)} %get-tuple-element.8.dx_ref, f32[2048,1024]{1,0:T(8,128)S(1)} %get-tuple-element.9.dw_ref), custom_call_target="tpu_custom_call" | custom-call | bytes 50331648 | tf_op jit(solution)/shard_map/pallas_call | solution.py:642
  285.9 0.0 collective-permute-done.1.tail_y_ref
  286.0 0.1 collective-permute-done.tail_ref
  286.1 0.8 shard_map.52
Async XLA Ops:
  275.4 10.6 %collective-permute-start = (f32[352,256]{1,0:T(8,128)}, f32[352,256]{1,0:T(8,128)S(1)}, u32[]{:S(2)}, u32[]{:S(2)}) collective-permute-start(f32[352,256]{1,0:T(8,128)} %get-tuple-element.12), channel_id=1, source_target_pairs={{0,2},{1,3},{2,0},{3,1},{4,6},{5,7},{6,4},{7,5}} | collective-permute-start | bytes 1081352 | tf_op jit(solution)/shard_map/ppermute | solution.py:640
  275.6 10.4 %collective-permute-start.1 = (f32[128,256]{1,0:T(8,128)}, f32[128,256]{1,0:T(8,128)S(1)}, u32[]{:S(2)}, u32[]{:S(2)}) collective-permute-start(f32[128,256]{1,0:T(8,128)} %get-tuple-element.13), channel_id=1, source_target_pairs={{0,4},{4,0},{1,5},{5,1},{2,6},{6,2},{3,7},{7,3}} | collective-permute-start | bytes 393224 | tf_op jit(solution)/shard_map/ppermute | solution.py:641

commit v10 on v9

--- a/solution.py
+++ b/solution.py
@@ -9,8 +9,8 @@
 F32 = jnp.float32
 BF16 = jnp.bfloat16
 H, N, D, T, Q, S = 2048, 1024, 512, 256, 128, 64
-R = 352
-E = 128
+R = 384
+E = 96
 F = D - E - R
 ME, SIB = 0, 1
 OWN, OTH = 0, 1

time: 287 us -> 287 us (level)
  transfers between devices with their start and end apart: 2 -> 2, of which waited for: 1 -> 0; matrix products, arithmetic and copies ran while one was open for 0% -> 0% of each run, Pallas kernels for 3% -> 3%
where the time goes in v10:
time: 287 us
  Pallas kernels  284 us (99%)
    pallas_call x1, Pallas kernels, local_backward(): pl.pallas_call(kernel, out_shape=(pltpu.VMEM((H, 2 * H), BF16), pltpu.VME...  275 us
    pallas_call x1, Pallas kernels, local_backward(): pl.pallas_call(store_kernel, out_shape=(jax.ShapeDtypeStruct((H, 2 * H),...  8.44 us
  transfers between devices with their start and end apart: 2, of which 0 were waited for; matrix products, arithmetic and copies ran while one was open for 0% of the time, Pallas kernels for 3%

profile of v10, /device:TPU:0, one launch (start us, length us, event | category | flops | bytes accessed | tf_op | source)
XLA Modules:
  0.0 286.8 jit_solution(18128096800725930224)
XLA Ops:
  0.6 274.8 %shard_map.50 = (bf16[2048,4096]{1,0:T(8,128)(2,1)S(1)}, f32[2048,1024]{1,0:T(8,128)S(1)}, bf16[2,2,2048,1024]{3,2,1,0:T(8,128)(2,1)}, f32[2,4,512,256]{3,2,1,0:...) custom-call(bf16[2048,4096]{1,0:T(8,128)(2,1)} %x_ref.1, bf16[2048,1024]{1,0:T(8,128)(2,1)} %w_ref.1, ...), custom_call_target="tpu_custom_call" | custom-call | flops 68719476736 | bytes 104857600 | tf_op jit(solution)/shard_map/pallas_call | solution.py:610
  275.4 0.8 collective-permute-start
  276.3 1.2 collective-permute-start.1
  277.5 8.4 %shard_map.51 = (bf16[2048,4096]{1,0:T(8,128)(2,1)}, f32[2048,1024]{1,0:T(8,128)}) custom-call(bf16[2048,4096]{1,0:T(8,128)(2,1)S(1)} %get-tuple-element.8.dx_ref, f32[2048,1024]{1,0:T(8,128)S(1)} %get-tuple-element.9.dw_ref), custom_call_target="tpu_custom_call" | custom-call | bytes 50331648 | tf_op jit(solution)/shard_map/pallas_call | solution.py:642
  285.9 0.0 collective-permute-done.1.tail_y_ref
  285.9 0.0 collective-permute-done.tail_ref
  285.9 0.8 shard_map.52
Async XLA Ops:
  275.4 10.5 %collective-permute-start = (f32[384,256]{1,0:T(8,128)}, f32[384,256]{1,0:T(8,128)S(1)}, u32[]{:S(2)}, u32[]{:S(2)}) collective-permute-start(f32[384,256]{1,0:T(8,128)} %get-tuple-element.12), channel_id=1, source_target_pairs={{0,2},{1,3},{2,0},{3,1},{4,6},{5,7},{6,4},{7,5}} | collective-permute-start | bytes 1179656 | tf_op jit(solution)/shard_map/ppermute | solution.py:640
  276.3 9.7 %collective-permute-start.1 = (f32[96,256]{1,0:T(8,128)}, f32[96,256]{1,0:T(8,128)S(1)}, u32[]{:S(2)}, u32[]{:S(2)}) collective-permute-start(f32[96,256]{1,0:T(8,128)} %get-tuple-element.13), channel_id=1, source_target_pairs={{0,4},{4,0},{1,5},{5,1},{2,6},{6,2},{3,7},{7,3}} | collective-permute-start | bytes 294920 | tf_op jit(solution)/shard_map/ppermute | solution.py:641

commit v11 on v10

--- a/solution.py
+++ b/solution.py
@@ -10,7 +10,8 @@
 BF16 = jnp.bfloat16
 H, N, D, T, Q, S = 2048, 1024, 512, 256, 128, 64
 R = 384
-E = 96
+E = 112
+EY = 72
 F = D - E - R
 ME, SIB = 0, 1
 OWN, OTH = 0, 1
@@ -43,7 +44,7 @@
     dx_ref, dw_ref, wbuf, bufy, tail, tail_y,
     dyv, pown, poth, wv, land, extra, swap,
     dy_sem, x_sem, dys_r, dyy_r, xs_r, xf_r, w_r, wp_r, ws_r, pa_r, ph_r, po_r, ps_r, py_r, pf_r,
-    s_dys, s_dyy, s_xs, s_w, s_ws, s_px, s_po, s_py, s_sum, wl_sem, tail_sem, tail_y_sem, s_ex, ex_r, py_ex, dyq_sem, xt_sem, xq_sem, s_sw, sw_r,
+    s_dys, s_dyy, s_xs, s_w, s_ws, s_px, s_po, s_py, s_sum, wl_sem, tail_sem, tail_y_sem, s_ex, ex_r, py_ex, dyq_sem, xt_sem, xq_sem, s_sw, sw_r, s_last,
 ):
     row = lax.axis_index("row")
     y = lax.axis_index("col")
@@ -141,7 +142,7 @@
 
     def p_own_last():
         return remote(
-            pown.at[3, 3, pl.ds(0, D - R)], dw_part(3, 3 * D, D - R), s_px, po_r.at[1, 3], xn
+            pown.at[3, 3, pl.ds(0, D - R)], dw_part(3, 3 * D, D - R), s_sum, po_r.at[1, 3], xn
         )
 
     def tail_store():
@@ -160,14 +161,14 @@
 
     def p_trans_short():
         part = pl.ds(0, F)
-        return remote(poth.at[1, 3, part], bufy.at[1, 3, part], s_py, pf_r.at[1, 12], yn)
+        return remote(poth.at[1, 3, part], bufy.at[1, 3, part], s_last, pf_r.at[1, 12], yn)
 
     def p_fwd_short():
         part = pl.ds(0, F)
-        return remote(bufy.at[1, 3, part], land.at[1, 3, part], s_px, pf_r.at[1, 12], xn)
+        return remote(bufy.at[1, 3, part], land.at[1, 3, part], s_last, pf_r.at[1, 12], xn)
 
     def p_trans_tail():
-        return remote(poth.at[1, 3, pl.ds(F, R)], tail, s_py, pf_r.at[1, 13], yn)
+        return remote(poth.at[1, 3, pl.ds(F, R)], tail, s_last, pf_r.at[1, 13], yn)
 
     def p_extra():
         return remote(poth.at[1, 3, pl.ds(D - E, E)], extra, s_ex, ex_r, xn)
@@ -183,11 +184,11 @@
         return remote(poth.at[1, 3, part], dw_part(1, 3 * D, D - E), s_py, py_r.at[1, 3], yn)
 
     def sum_short():
-        part = pl.ds(0, D - E)
-        return remote(poth.at[3, 3, part], dw_part(3, 3 * D, D - E), s_sum, py_r.at[3, 3], yn)
+        part = pl.ds(0, D - EY)
+        return remote(poth.at[3, 3, part], dw_part(3, 3 * D, D - EY), s_last, py_r.at[3, 3], yn)
 
     def tail_y_store(src):
-        return local(src.at[3, 3, pl.ds(D - E, E)], tail_y, tail_y_sem)
+        return local(src.at[3, 3, pl.ds(D - EY, EY)], tail_y, tail_y_sem)
 
     def sum_to_y(q, kt):
         return remote(poth.at[q, kt], dw_tile(q, kt), s_sum, py_r.at[q, kt], yn)
@@ -503,9 +504,10 @@
         top[...] = top[...] + pown[3, 3, :D - R]
         drain(wbuf.at[ME], s_w)
         tail_y_store(poth).wait()
-        drain(dyv.at[ME, OWN, pl.ds(0, H - (E + R) // 2)], s_px)
+        drain(dyv.at[ME, OWN, pl.ds(0, H - T)], s_px)
         drain(land, s_py)
-        drain(dyv.at[ME, OWN, pl.ds(0, H - E // 2)], s_sum)
+        drain(dyv.at[ME, OWN, pl.ds(0, H - T)], s_sum)
+        drain(land.at[0, 0, pl.ds(0, D - EY + F)], s_last)
 
     @pl.when(is_b)
     def _():
@@ -564,10 +566,12 @@
         tail_y_store(pown).wait()
         tail_store().wait()
         drain(wbuf.at[ME, OWN], s_w)
-        drain(dw_ref.at[pl.ds(0, H - R // 4)], s_px)
+        drain(dw_ref.at[pl.ds(0, H - Q)], s_px)
+        drain(land.at[0, 0, pl.ds(0, D - R)], s_sum)
+        drain(land.at[0, 0, pl.ds(0, D - E)], s_last)
         drain(land, s_po)
         drain(extra, s_ex)
-        drain(dyv.at[ME, OWN, pl.ds(0, H - E // 2)], s_py)
+        drain(dyv.at[ME, OWN, pl.ds(0, H - T)], s_py)
 
     drain(dyv.at[ME], s_dys)
     drain(dyv.at[ME, OWN], s_dyy)
@@ -590,12 +594,12 @@
 
 def add_kernel(done_ref, dw_ref, tail_ref, tail_y_ref, dw_out, buf, buf_y, sem, sem_y):
     is_a = lax.axis_index("row") // 2 == lax.axis_index("col")
-    rows = cut(jnp.where(is_a, H - R, 3 * D + F), R, 32)
+    rows = cut(jnp.where(is_a, H - R, 3 * D + F), R, 16)
     cols = cut(jnp.where(is_a, 3 * T, T), T)
     buf[...] = dw_ref[rows, cols] + tail_ref[...]
     first = pltpu.make_async_copy(buf, dw_out.at[rows, cols], sem)
     first.start()
-    rows_y, cols_y = pl.ds(H - E, E), cut(jnp.where(is_a, 0, 3 * T), T)
+    rows_y, cols_y = pl.ds(H - EY, EY), cut(jnp.where(is_a, 0, 3 * T), T)
     buf_y[...] = jnp.where(is_a, dw_ref[rows_y, cols_y], tail_y_ref[...])
     second = pltpu.make_async_copy(buf_y, dw_out.at[rows_y, cols_y], sem_y)
     second.start()
@@ -615,7 +619,7 @@
             jax.ShapeDtypeStruct((2, 2, H, N), BF16),
             jax.ShapeDtypeStruct((2, 4, D, T), F32),
             jax.ShapeDtypeStruct((R, T), F32),
-            jax.ShapeDtypeStruct((E, T), F32),
+            jax.ShapeDtypeStruct((EY, T), F32),
         ),
         in_specs=[any_spec] * 3,
         out_specs=(vmem_spec,) * 2 + (any_spec,) * 4,
@@ -630,7 +634,7 @@
             dma, dma((4,)), dma((2, 4)), dma((4,)), dma((4,)), dma((5,)), dma((2, 8)), dma((16,)), dma((2, 8)),
             dma((4,)), dma((2, 8)), dma((2, 4)), dma((2, 4)), dma((4, 4)), dma((2, 16)),
             dma, dma, dma, dma, dma, dma, dma, dma, dma, dma((2, 2)), dma,
-            dma, dma, dma, dma, dma, dma, dma, dma, dma,
+            dma, dma, dma, dma, dma, dma, dma, dma, dma, dma,
         ],
         compiler_params=pltpu.CompilerParams(
             collective_id=0, has_side_effects=True, vmem_limit_bytes=41_800_000
@@ -653,7 +657,7 @@
         out_shape=jax.ShapeDtypeStruct((H, N), F32),
         in_specs=[any_spec] + [vmem_spec] * 3,
         out_specs=any_spec,
-        scratch_shapes=[pltpu.VMEM((R, T), F32), pltpu.VMEM((E, T), F32), dma, dma],
+        scratch_shapes=[pltpu.VMEM((R, T), F32), pltpu.VMEM((EY, T), F32), dma, dma],
         input_output_aliases={0: 0},
         compiler_params=pltpu.CompilerParams(vmem_limit_bytes=2 << 20),
         cost_estimate=pl.CostEstimate(flops=0, bytes_accessed=1 << 20, transcendentals=0),

time: 287 us -> 287 us (level)
  transfers between devices with their start and end apart: 2 -> 2, of which waited for: 0 -> 1; matrix products, arithmetic and copies ran while one was open for 0% -> 0% of each run, Pallas kernels for 3% -> 3%
where the time goes in v11:
time: 287 us
  Pallas kernels  284 us (99%)
    pallas_call x1, Pallas kernels, local_backward(): pl.pallas_call(kernel, out_shape=(pltpu.VMEM((H, 2 * H), BF16), pltpu.VME...  274 us
    pallas_call x1, Pallas kernels, local_backward(): pl.pallas_call(store_kernel, out_shape=(jax.ShapeDtypeStruct((H, 2 * H),...  8.44 us
  transfers between devices with their start and end apart: 2, of which 1 were waited for; matrix products, arithmetic and copies ran while one was open for 0% of the time, Pallas kernels for 3%

profile of v11, /device:TPU:0, one launch (start us, length us, event | category | flops | bytes accessed | tf_op | source)
XLA Modules:
  0.0 286.7 jit_solution(12336658945765034574)
XLA Ops:
  0.6 274.4 %shard_map.50 = (bf16[2048,4096]{1,0:T(8,128)(2,1)S(1)}, f32[2048,1024]{1,0:T(8,128)S(1)}, bf16[2,2,2048,1024]{3,2,1,0:T(8,128)(2,1)}, f32[2,4,512,256]{3,2,1,0:...) custom-call(bf16[2048,4096]{1,0:T(8,128)(2,1)} %x_ref.1, bf16[2048,1024]{1,0:T(8,128)(2,1)} %w_ref.1, ...), custom_call_target="tpu_custom_call" | custom-call | flops 68719476736 | bytes 104857600 | tf_op jit(solution)/shard_map/pallas_call | solution.py:614
  275.1 1.7 collective-permute-start
  276.8 0.3 collective-permute-start.1
  277.1 8.4 %shard_map.51 = (bf16[2048,4096]{1,0:T(8,128)(2,1)}, f32[2048,1024]{1,0:T(8,128)}) custom-call(bf16[2048,4096]{1,0:T(8,128)(2,1)S(1)} %get-tuple-element.8.dx_ref, f32[2048,1024]{1,0:T(8,128)S(1)} %get-tuple-element.9.dw_ref), custom_call_target="tpu_custom_call" | custom-call | bytes 50331648 | tf_op jit(solution)/shard_map/pallas_call | solution.py:646
  285.6 0.0 collective-permute-done.1.tail_y_ref
  285.6 0.2 collective-permute-done.tail_ref
  285.8 0.8 shard_map.52
Async XLA Ops:
  275.1 10.7 %collective-permute-start = (f32[384,256]{1,0:T(8,128)}, f32[384,256]{1,0:T(8,128)S(1)}, u32[]{:S(2)}, u32[]{:S(2)}) collective-permute-start(f32[384,256]{1,0:T(8,128)} %get-tuple-element.12), channel_id=1, source_target_pairs={{0,2},{1,3},{2,0},{3,1},{4,6},{5,7},{6,4},{7,5}} | collective-permute-start | bytes 1179656 | tf_op jit(solution)/shard_map/ppermute | solution.py:644
  276.8 8.8 %collective-permute-start.1 = (f32[72,256]{1,0:T(8,128)}, f32[72,256]{1,0:T(8,128)S(1)}, u32[]{:S(2)}, u32[]{:S(2)}) collective-permute-start(f32[72,256]{1,0:T(8,128)} %get-tuple-element.13), channel_id=1, source_target_pairs={{0,4},{4,0},{1,5},{5,1},{2,6},{6,2},{3,7},{7,3}} | collective-permute-start | bytes 221192 | tf_op jit(solution)/shard_map/ppermute | solution.py:645

commit v12 on v11

--- a/solution.py
+++ b/solution.py
@@ -9,14 +9,14 @@
 F32 = jnp.float32
 BF16 = jnp.bfloat16
 H, N, D, T, Q, S = 2048, 1024, 512, 256, 128, 64
-R = 384
+R = 368
 E = 112
 EY = 72
 F = D - E - R
 ME, SIB = 0, 1
 OWN, OTH = 0, 1
 ARG, BUF = "arg", "buf"
-FIRST = ((0, T), (T, T))
+FIRST = ((0, Q), (Q, Q), (T, T))
 
 
 def _tdot(a, b):
@@ -81,11 +81,17 @@
 
     dyq_load = local(dy_ref.at[:, pl.ds(0, T)], dyv.at[ME, OWN, :, pl.ds(0, T)], dyq_sem)
     dy_load = local(dy_ref.at[:, pl.ds(T, N - T)], dyv.at[ME, OWN, :, pl.ds(T, N - T)], dy_sem)
-    xt_load = local(x_ref.at[:, pl.ds((1 - c) * H, T)], xo(3 * D, T), xt_sem)
-    xq_load = local(x_ref.at[:, pl.ds(c * H, T)], xo(0, T), xq_sem)
+    def xt_load(h):
+        return local(x_ref.at[:, pl.ds((1 - c) * H + h * Q, Q)], xo(3 * D + h * Q, Q), xt_sem.at[h])
+
+    def xq_load(h):
+        return local(x_ref.at[:, pl.ds(c * H + h * Q, Q)], xo(h * Q, Q), xq_sem.at[h])
+
+    def swap_part(h):
+        part = pl.ds(h * Q, Q)
+        return remote(swap.at[0, part], swap.at[1, part], s_sw, sw_r.at[h], sib)
+
     x0_load = local(x_ref.at[:, pl.ds(c * H + T, D - T)], xo(T, D - T), x_sem.at[0])
-    swap_part = remote(swap.at[0], swap.at[1], s_sw, sw_r, sib)
-
     def x_load(kt):
         return local(x_ref.at[:, pl.ds(c * H + kt * D, D)], xo(kt * D, D), x_sem.at[kt])
 
@@ -96,8 +102,7 @@
         return x_cols_to_sib(kt * D, D, xs_r.at[kt])
 
     def x_first(i):
-        k0, n = FIRST[i]
-        return x_cols_to_sib(k0, n, xf_r.at[i])
+        return x_cols_to_sib(i * T, T, xf_r.at[i])
 
     def dy_to_sib(j, q):
         src = dy_ref.at[:, qs(q)] if j == OWN else dyv.at[ME, OTH, :, qs(q)]
@@ -196,7 +201,7 @@
     def drain(ref, sem):
         remote(ref, ref, sem, dyy_r.at[0], yn).wait_send()
 
-    for cp in (dyq_load, xt_load, xq_load):
+    for cp in (dyq_load, xt_load(0), xq_load(0)):
         cp.start()
 
     barrier = pltpu.get_barrier_semaphore()
@@ -223,14 +228,36 @@
         for p in range(16):
             w_to_y_piece(p).start()
 
+    def swap_send(h):
+        xt_load(h).wait()
+        xq_load(h).wait()
+        if h == 0:
+            xt_load(1).start()
+            xq_load(1).start()
+        swap[0, pl.ds(h * Q, Q)] = _tdot(dx_ref[:, 3 * D + h * Q:3 * D + h * Q + Q], dyv[ME, OWN, :, :T])
+        swap_part(h).start()
+
+    def own_first(h):
+        pown[0, 0, pl.ds(h * Q, Q)] = _tdot(dx_ref[:, h * Q:h * Q + Q], dyv[ME, OWN, :, :T])
+
+    def swap_add(h):
+        part = pl.ds(h * Q, Q)
+        swap_part(h).wait_recv()
+        pown[0, 0, part] = pown[0, 0, part] + swap[1, part]
+
+        @pl.when(is_b)
+        def _():
+            p_first(h).start()
+
     dyq_load.wait()
-    xt_load.wait()
-    xq_load.wait()
-    swap[0] = _tdot(dx_ref[:, 3 * D:3 * D + T], dyv[ME, OWN, :, :T])
-    swap_part.start()
+    swap_send(0)
+    own_first(0)
+    swap_send(1)
     dy_to_sib(OWN, 0).start()
     x_first(1).start()
-    pown[0, 0, :T] = _tdot(dx_ref[:, :T], dyv[ME, OWN, :, :T])
+    swap_add(0)
+    own_first(1)
+    swap_add(1)
     for cp in (x0_load, dy_load, x_load(1), x_load(2), x_load(3)):
         cp.start()
     x_first(0).start()
@@ -243,13 +270,6 @@
     def _():
         for i in range(8):
             w_to_sib(OWN, i, ARG).start()
-
-    swap_part.wait_recv()
-    pown[0, 0, :T] = pown[0, 0, :T] + swap[1]
-
-    @pl.when(is_b)
-    def _():
-        p_first(0).start()
 
     def p_part(j, c0, k0, n):
         dy = pl.ds(c0, T)
@@ -274,7 +294,7 @@
 
     @pl.when(is_b)
     def _():
-        p_first(1).start()
+        p_first(2).start()
 
     x_first(0).wait_recv()
     dy_load.wait()
@@ -634,7 +654,7 @@
             dma, dma((4,)), dma((2, 4)), dma((4,)), dma((4,)), dma((5,)), dma((2, 8)), dma((16,)), dma((2, 8)),
             dma((4,)), dma((2, 8)), dma((2, 4)), dma((2, 4)), dma((4, 4)), dma((2, 16)),
             dma, dma, dma, dma, dma, dma, dma, dma, dma, dma((2, 2)), dma,
-            dma, dma, dma, dma, dma, dma, dma, dma, dma, dma,
+            dma, dma, dma, dma, dma, dma((2,)), dma((2,)), dma, dma((2,)), dma,
         ],
         compiler_params=pltpu.CompilerParams(
             collective_id=0, has_side_effects=True, vmem_limit_bytes=41_800_000

time: 287 us -> 287 us (level)
  transfers between devices with their start and end apart: 2 -> 2, of which waited for: 1 -> 0; matrix products, arithmetic and copies ran while one was open for 0% -> 0% of each run, Pallas kernels for 3% -> 3%
where the time goes in v12:
time: 287 us
  Pallas kernels  284 us (99%)
    pallas_call x1, Pallas kernels, local_backward(): pl.pallas_call(kernel, out_shape=(pltpu.VMEM((H, 2 * H), BF16), pltpu.VME...  275 us
    pallas_call x1, Pallas kernels, local_backward(): pl.pallas_call(store_kernel, out_shape=(jax.ShapeDtypeStruct((H, 2 * H),...  8.44 us
  transfers between devices with their start and end apart: 2, of which 0 were waited for; matrix products, arithmetic and copies ran while one was open for 0% of the time, Pallas kernels for 3%

profile of v12, /device:TPU:0, one launch (start us, length us, event | category | flops | bytes accessed | tf_op | source)
XLA Modules:
  0.0 286.8 jit_solution(7954959141876744799)
XLA Ops:
  0.6 274.6 %shard_map.50 = (bf16[2048,4096]{1,0:T(8,128)(2,1)S(1)}, f32[2048,1024]{1,0:T(8,128)S(1)}, bf16[2,2,2048,1024]{3,2,1,0:T(8,128)(2,1)}, f32[2,4,512,256]{3,2,1,0:...) custom-call(bf16[2048,4096]{1,0:T(8,128)(2,1)} %x_ref.1, bf16[2048,1024]{1,0:T(8,128)(2,1)} %w_ref.1, ...), custom_call_target="tpu_custom_call" | custom-call | flops 68719476736 | bytes 104857600 | tf_op jit(solution)/shard_map/pallas_call | solution.py:634
  275.3 1.5 collective-permute-start
  276.8 0.5 collective-permute-start.1
  277.3 8.4 %shard_map.51 = (bf16[2048,4096]{1,0:T(8,128)(2,1)}, f32[2048,1024]{1,0:T(8,128)}) custom-call(bf16[2048,4096]{1,0:T(8,128)(2,1)S(1)} %get-tuple-element.8.dx_ref, f32[2048,1024]{1,0:T(8,128)S(1)} %get-tuple-element.9.dw_ref), custom_call_target="tpu_custom_call" | custom-call | bytes 50331648 | tf_op jit(solution)/shard_map/pallas_call | solution.py:666
  285.8 0.0 collective-permute-done.1.tail_y_ref
  285.8 0.0 collective-permute-done.tail_ref
  285.8 0.8 shard_map.52
Async XLA Ops:
  275.3 10.5 %collective-permute-start = (f32[368,256]{1,0:T(8,128)}, f32[368,256]{1,0:T(8,128)S(1)}, u32[]{:S(2)}, u32[]{:S(2)}) collective-permute-start(f32[368,256]{1,0:T(8,128)} %get-tuple-element.12), channel_id=1, source_target_pairs={{0,2},{1,3},{2,0},{3,1},{4,6},{5,7},{6,4},{7,5}} | collective-permute-start | bytes 1130504 | tf_op jit(solution)/shard_map/ppermute | solution.py:664
  276.8 9.0 %collective-permute-start.1 = (f32[72,256]{1,0:T(8,128)}, f32[72,256]{1,0:T(8,128)S(1)}, u32[]{:S(2)}, u32[]{:S(2)}) collective-permute-start(f32[72,256]{1,0:T(8,128)} %get-tuple-element.13), channel_id=1, source_target_pairs={{0,4},{4,0},{1,5},{5,1},{2,6},{6,2},{3,7},{7,3}} | collective-permute-start | bytes 221192 | tf_op jit(solution)/shard_map/ppermute | solution.py:665

commit v13 on v12

--- a/solution.py
+++ b/solution.py
@@ -9,9 +9,9 @@
 F32 = jnp.float32
 BF16 = jnp.bfloat16
 H, N, D, T, Q, S = 2048, 1024, 512, 256, 128, 64
-R = 368
+R = 376
 E = 112
-EY = 72
+EY = 96
 F = D - E - R
 ME, SIB = 0, 1
 OWN, OTH = 0, 1
@@ -602,10 +602,12 @@
 
 def store_kernel(dx_ref, dw_ref, dx_out, dw_out, sem):
     copies = []
-    for i in range(4):
-        part = pl.ds(i * D, D)
+    for i in range(16):
+        part = pl.ds(i * Q, Q)
         copies.append(pltpu.make_async_copy(dx_ref.at[part], dx_out.at[part], sem.at[0, i]))
-        copies.append(pltpu.make_async_copy(dw_ref.at[part], dw_out.at[part], sem.at[1, i]))
+        if i % 2:
+            part = pl.ds((i - 1) * Q, T)
+            copies.append(pltpu.make_async_copy(dw_ref.at[part], dw_out.at[part], sem.at[1, i]))
     for cp in copies:
         cp.start()
     for cp in copies:
@@ -614,7 +616,7 @@
 
 def add_kernel(done_ref, dw_ref, tail_ref, tail_y_ref, dw_out, buf, buf_y, sem, sem_y):
     is_a = lax.axis_index("row") // 2 == lax.axis_index("col")
-    rows = cut(jnp.where(is_a, H - R, 3 * D + F), R, 16)
+    rows = cut(jnp.where(is_a, H - R, 3 * D + F), R, 8)
     cols = cut(jnp.where(is_a, 3 * T, T), T)
     buf[...] = dw_ref[rows, cols] + tail_ref[...]
     first = pltpu.make_async_copy(buf, dw_out.at[rows, cols], sem)
@@ -668,7 +670,7 @@
         out_shape=(jax.ShapeDtypeStruct((H, 2 * H), BF16), jax.ShapeDtypeStruct((H, N), F32)),
         in_specs=[vmem_spec] * 2,
         out_specs=(any_spec,) * 2,
-        scratch_shapes=[dma((2, 4))],
+        scratch_shapes=[dma((2, 16))],
         compiler_params=pltpu.CompilerParams(vmem_limit_bytes=1 << 20),
         cost_estimate=pl.CostEstimate(flops=0, bytes_accessed=48 << 20, transcendentals=0),
     )(outs[0], outs[1])

time: 287 us -> 287 us (level)
  no operation moved by 1% of the time
where the time goes in v13:
time: 287 us
  Pallas kernels  284 us (99%)
    pallas_call x1, Pallas kernels, local_backward(): pl.pallas_call(kernel, out_shape=(pltpu.VMEM((H, 2 * H), BF16), pltpu.VME...  275 us
    pallas_call x1, Pallas kernels, local_backward(): pl.pallas_call(store_kernel, out_shape=(jax.ShapeDtypeStruct((H, 2 * H),...  8.62 us
  transfers between devices with their start and end apart: 2, of which 0 were waited for; matrix products, arithmetic and copies ran while one was open for 0% of the time, Pallas kernels for 3%

profile of v13, /device:TPU:0, one launch (start us, length us, event | category | flops | bytes accessed | tf_op | source)
XLA Modules:
  0.0 287.0 jit_solution(16372689430731544129)
XLA Ops:
  0.6 274.6 %shard_map.50 = (bf16[2048,4096]{1,0:T(8,128)(2,1)S(1)}, f32[2048,1024]{1,0:T(8,128)S(1)}, bf16[2,2,2048,1024]{3,2,1,0:T(8,128)(2,1)}, f32[2,4,512,256]{3,2,1,0:...) custom-call(bf16[2048,4096]{1,0:T(8,128)(2,1)} %x_ref.1, bf16[2048,1024]{1,0:T(8,128)(2,1)} %w_ref.1, ...), custom_call_target="tpu_custom_call" | custom-call | flops 68719476736 | bytes 104857600 | tf_op jit(solution)/shard_map/pallas_call | solution.py:636
  275.3 1.0 collective-permute-start
  276.3 1.0 collective-permute-start.1
  277.3 8.6 %shard_map.51 = (bf16[2048,4096]{1,0:T(8,128)(2,1)}, f32[2048,1024]{1,0:T(8,128)}) custom-call(bf16[2048,4096]{1,0:T(8,128)(2,1)S(1)} %get-tuple-element.8.dx_ref, f32[2048,1024]{1,0:T(8,128)S(1)} %get-tuple-element.9.dw_ref), custom_call_target="tpu_custom_call" | custom-call | bytes 50331648 | tf_op jit(solution)/shard_map/pallas_call | solution.py:668
  286.0 0.0 collective-permute-done.1.tail_y_ref
  286.0 0.0 collective-permute-done.tail_ref
  286.0 0.8 shard_map.52
Async XLA Ops:
  275.3 10.7 %collective-permute-start = (f32[376,256]{1,0:T(8,128)}, f32[376,256]{1,0:T(8,128)S(1)}, u32[]{:S(2)}, u32[]{:S(2)}) collective-permute-start(f32[376,256]{1,0:T(8,128)} %get-tuple-element.12), channel_id=1, source_target_pairs={{0,2},{1,3},{2,0},{3,1},{4,6},{5,7},{6,4},{7,5}} | collective-permute-start | bytes 1155080 | tf_op jit(solution)/shard_map/ppermute | solution.py:666
  276.3 9.7 %collective-permute-start.1 = (f32[96,256]{1,0:T(8,128)}, f32[96,256]{1,0:T(8,128)S(1)}, u32[]{:S(2)}, u32[]{:S(2)}) collective-permute-start(f32[96,256]{1,0:T(8,128)} %get-tuple-element.13), channel_id=1, source_target_pairs={{0,4},{4,0},{1,5},{5,1},{2,6},{6,2},{3,7},{7,3}} | collective-permute-start | bytes 294920 | tf_op jit(solution)/shard_map/ppermute | solution.py:667

commit v14 on v13

--- a/solution.py
+++ b/solution.py
@@ -602,12 +602,10 @@
 
 def store_kernel(dx_ref, dw_ref, dx_out, dw_out, sem):
     copies = []
-    for i in range(16):
-        part = pl.ds(i * Q, Q)
+    for i in range(2):
+        part = pl.ds(i * N, N)
         copies.append(pltpu.make_async_copy(dx_ref.at[part], dx_out.at[part], sem.at[0, i]))
-        if i % 2:
-            part = pl.ds((i - 1) * Q, T)
-            copies.append(pltpu.make_async_copy(dw_ref.at[part], dw_out.at[part], sem.at[1, i]))
+        copies.append(pltpu.make_async_copy(dw_ref.at[part], dw_out.at[part], sem.at[1, i]))
     for cp in copies:
         cp.start()
     for cp in copies:
@@ -670,7 +668,7 @@
         out_shape=(jax.ShapeDtypeStruct((H, 2 * H), BF16), jax.ShapeDtypeStruct((H, N), F32)),
         in_specs=[vmem_spec] * 2,
         out_specs=(any_spec,) * 2,
-        scratch_shapes=[dma((2, 16))],
+        scratch_shapes=[dma((2, 2))],
         compiler_params=pltpu.CompilerParams(vmem_limit_bytes=1 << 20),
         cost_estimate=pl.CostEstimate(flops=0, bytes_accessed=48 << 20, transcendentals=0),
     )(outs[0], outs[1])

time: 287 us -> 287 us (level)
  no operation moved by 1% of the time
where the time goes in v14:
time: 287 us
  Pallas kernels  284 us (99%)
    pallas_call x1, Pallas kernels, local_backward(): pl.pallas_call(kernel, out_shape=(pltpu.VMEM((H, 2 * H), BF16), pltpu.VME...  275 us
    pallas_call x1, Pallas kernels, local_backward(): pl.pallas_call(store_kernel, out_shape=(jax.ShapeDtypeStruct((H, 2 * H),...  8.59 us
  transfers between devices with their start and end apart: 2, of which 0 were waited for; matrix products, arithmetic and copies ran while one was open for 0% of the time, Pallas kernels for 3%

profile of v14, /device:TPU:0, one launch (start us, length us, event | category | flops | bytes accessed | tf_op | source)
XLA Modules:
  0.0 287.0 jit_solution(1676633501621974756)
XLA Ops:
  0.6 274.6 %shard_map.50 = (bf16[2048,4096]{1,0:T(8,128)(2,1)S(1)}, f32[2048,1024]{1,0:T(8,128)S(1)}, bf16[2,2,2048,1024]{3,2,1,0:T(8,128)(2,1)}, f32[2,4,512,256]{3,2,1,0:...) custom-call(bf16[2048,4096]{1,0:T(8,128)(2,1)} %x_ref.1, bf16[2048,1024]{1,0:T(8,128)(2,1)} %w_ref.1, ...), custom_call_target="tpu_custom_call" | custom-call | flops 68719476736 | bytes 104857600 | tf_op jit(solution)/shard_map/pallas_call | solution.py:634
  275.3 1.0 collective-permute-start
  276.3 1.0 collective-permute-start.1
  277.3 8.6 %shard_map.51 = (bf16[2048,4096]{1,0:T(8,128)(2,1)}, f32[2048,1024]{1,0:T(8,128)}) custom-call(bf16[2048,4096]{1,0:T(8,128)(2,1)S(1)} %get-tuple-element.8.dx_ref, f32[2048,1024]{1,0:T(8,128)S(1)} %get-tuple-element.9.dw_ref), custom_call_target="tpu_custom_call" | custom-call | bytes 50331648 | tf_op jit(solution)/shard_map/pallas_call | solution.py:666
  285.9 0.0 collective-permute-done.1.tail_y_ref
  285.9 0.0 collective-permute-done.tail_ref
  286.0 0.8 shard_map.52
Async XLA Ops:
  275.3 10.7 %collective-permute-start = (f32[376,256]{1,0:T(8,128)}, f32[376,256]{1,0:T(8,128)S(1)}, u32[]{:S(2)}, u32[]{:S(2)}) collective-permute-start(f32[376,256]{1,0:T(8,128)} %get-tuple-element.12), channel_id=1, source_target_pairs={{0,2},{1,3},{2,0},{3,1},{4,6},{5,7},{6,4},{7,5}} | collective-permute-start | bytes 1155080 | tf_op jit(solution)/shard_map/ppermute | solution.py:664
  276.3 9.6 %collective-permute-start.1 = (f32[96,256]{1,0:T(8,128)}, f32[96,256]{1,0:T(8,128)S(1)}, u32[]{:S(2)}, u32[]{:S(2)}) collective-permute-start(f32[96,256]{1,0:T(8,128)} %get-tuple-element.13), channel_id=1, source_target_pairs={{0,4},{4,0},{1,5},{5,1},{2,6},{6,2},{3,7},{7,3}} | collective-permute-start | bytes 294920 | tf_op jit(solution)/shard_map/ppermute | solution.py:665

commit v15 on v12

--- a/solution.py
+++ b/solution.py
@@ -9,9 +9,9 @@
 F32 = jnp.float32
 BF16 = jnp.bfloat16
 H, N, D, T, Q, S = 2048, 1024, 512, 256, 128, 64
-R = 368
-E = 112
-EY = 72
+R = 376
+E = 120
+EY = 88
 F = D - E - R
 ME, SIB = 0, 1
 OWN, OTH = 0, 1
@@ -614,7 +614,7 @@
 
 def add_kernel(done_ref, dw_ref, tail_ref, tail_y_ref, dw_out, buf, buf_y, sem, sem_y):
     is_a = lax.axis_index("row") // 2 == lax.axis_index("col")
-    rows = cut(jnp.where(is_a, H - R, 3 * D + F), R, 16)
+    rows = cut(jnp.where(is_a, H - R, 3 * D + F), R, 8)
     cols = cut(jnp.where(is_a, 3 * T, T), T)
     buf[...] = dw_ref[rows, cols] + tail_ref[...]
     first = pltpu.make_async_copy(buf, dw_out.at[rows, cols], sem)

time: 287 us -> 287 us (level)
  no operation moved by 1% of the time
where the time goes in v15:
time: 287 us
  Pallas kernels  284 us (99%)
    pallas_call x1, Pallas kernels, local_backward(): pl.pallas_call(kernel, out_shape=(pltpu.VMEM((H, 2 * H), BF16), pltpu.VME...  274 us
    pallas_call x1, Pallas kernels, local_backward(): pl.pallas_call(store_kernel, out_shape=(jax.ShapeDtypeStruct((H, 2 * H),...  8.44 us
  transfers between devices with their start and end apart: 2, of which 0 were waited for; matrix products, arithmetic and copies ran while one was open for 0% of the time, Pallas kernels for 3%

profile of v15, /device:TPU:0, one launch (start us, length us, event | category | flops | bytes accessed | tf_op | source)
XLA Modules:
  0.0 286.6 jit_solution(657689121039570952)
XLA Ops:
  0.6 274.5 %shard_map.50 = (bf16[2048,4096]{1,0:T(8,128)(2,1)S(1)}, f32[2048,1024]{1,0:T(8,128)S(1)}, bf16[2,2,2048,1024]{3,2,1,0:T(8,128)(2,1)}, f32[2,4,512,256]{3,2,1,0:...) custom-call(bf16[2048,4096]{1,0:T(8,128)(2,1)} %x_ref.1, bf16[2048,1024]{1,0:T(8,128)(2,1)} %w_ref.1, ...), custom_call_target="tpu_custom_call" | custom-call | flops 68719476736 | bytes 104857600 | tf_op jit(solution)/shard_map/pallas_call | solution.py:634
  275.1 1.4 collective-permute-start
  276.5 0.7 collective-permute-start.1
  277.2 8.4 %shard_map.51 = (bf16[2048,4096]{1,0:T(8,128)(2,1)}, f32[2048,1024]{1,0:T(8,128)}) custom-call(bf16[2048,4096]{1,0:T(8,128)(2,1)S(1)} %get-tuple-element.8.dx_ref, f32[2048,1024]{1,0:T(8,128)S(1)} %get-tuple-element.9.dw_ref), custom_call_target="tpu_custom_call" | custom-call | bytes 50331648 | tf_op jit(solution)/shard_map/pallas_call | solution.py:666
  285.6 0.0 collective-permute-done.1.tail_y_ref
  285.6 0.0 collective-permute-done.tail_ref
  285.6 0.8 shard_map.52
Async XLA Ops:
  275.1 10.5 %collective-permute-start = (f32[376,256]{1,0:T(8,128)}, f32[376,256]{1,0:T(8,128)S(1)}, u32[]{:S(2)}, u32[]{:S(2)}) collective-permute-start(f32[376,256]{1,0:T(8,128)} %get-tuple-element.12), channel_id=1, source_target_pairs={{0,2},{1,3},{2,0},{3,1},{4,6},{5,7},{6,4},{7,5}} | collective-permute-start | bytes 1155080 | tf_op jit(solution)/shard_map/ppermute | solution.py:664
  276.5 9.1 %collective-permute-start.1 = (f32[88,256]{1,0:T(8,128)}, f32[88,256]{1,0:T(8,128)S(1)}, u32[]{:S(2)}, u32[]{:S(2)}) collective-permute-start(f32[88,256]{1,0:T(8,128)} %get-tuple-element.13), channel_id=1, source_target_pairs={{0,4},{4,0},{1,5},{5,1},{2,6},{6,2},{3,7},{7,3}} | collective-permute-start | bytes 270344 | tf_op jit(solution)/shard_map/ppermute | solution.py:665
